TPU v7x, 8 devices: a whole 2x2x1 slice. The times are simulated.
8 devices in a mesh: ens: 1 (over z), col: 2 (over y), row: 4 (over x, core).
Axes of the slice: x: 2, y: 2, z: 1, core: 2. Of those that a mesh axis runs over, the one named last changes fastest.
Arguments:
- vel_re: float32 [64, 3, 32, 32, 16], P('ens', None, None, 'row', 'col')
- vel_im: float32 [64, 3, 32, 32, 16], P('ens', None, None, 'row', 'col')
- scal_re: float32 [64, 32, 32, 16], P('ens', None, 'row', 'col')
- scal_im: float32 [64, 32, 32, 16], P('ens', None, 'row', 'col')
Outputs:
- output 1: float32 [64, 3, 32, 32, 16], P('ens', None, None, 'row', 'col')
- output 2: float32 [64, 3, 32, 32, 16], P('ens', None, None, 'row', 'col')
- output 3: float32 [64, 32, 32, 16], P('ens', None, 'row', 'col')
- output 4: float32 [64, 32, 32, 16], P('ens', None, 'row', 'col')
All inputs are finite; a program needn't handle non-finite values.
Results may differ from a plain program's by a relative error of at most 0.001.
Values are sent between devices in bfloat16 or wider.
A program may use at most 1 GiB of HBM per device.

v0:
```python
import math
import jax
import jax.numpy as jnp
from jax import lax
from jax.sharding import PartitionSpec as P

TWO_PI = 2.0 * math.pi


def wave_numbers(grid_n, y_start, y_count, z_start, z_count):
    index_x = jnp.arange(grid_n)
    index_y = y_start + jnp.arange(y_count)
    modes_x = jnp.where(index_x < grid_n // 2, index_x, index_x - grid_n)
    modes_y = jnp.where(index_y < grid_n // 2, index_y, index_y - grid_n)
    modes_z = z_start + jnp.arange(z_count)
    k_scale = TWO_PI / grid_n
    k_x = (modes_x * k_scale).astype(jnp.float32)[:, None, None]
    k_y = (modes_y * k_scale).astype(jnp.float32)[None, :, None]
    k_z = (modes_z * k_scale).astype(jnp.float32)[None, None, :]
    k_sq = k_x * k_x + k_y * k_y + k_z * k_z
    band_x = (3 * jnp.abs(modes_x) < grid_n)[:, None, None]
    band_y = (3 * jnp.abs(modes_y) < grid_n)[None, :, None]
    band_z = (3 * modes_z < grid_n)[None, None, :]
    keep_mask = band_x & band_y & band_z & (k_sq > 0)
    return k_x, k_y, k_z, k_sq, keep_mask


def spectral_fields(vel_hat, scal_hat, waves):
    k_x, k_y, k_z = waves[0], waves[1], waves[2]
    u_x, u_y, u_z = vel_hat[:, 0], vel_hat[:, 1], vel_hat[:, 2]
    return jnp.stack([u_x, u_y, u_z, 1j * (k_y * u_z - k_z * u_y), 1j * (k_z * u_x - k_x * u_z), 1j * (k_x * u_y - k_y * u_x), scal_hat], axis=1)


def grid_products(physical):
    v_x, v_y, v_z = physical[:, 0], physical[:, 1], physical[:, 2]
    w_x, w_y, w_z = physical[:, 3], physical[:, 4], physical[:, 5]
    scalar_field = physical[:, 6]
    return jnp.stack([v_y * w_z - v_z * w_y, v_z * w_x - v_x * w_z, v_x * w_y - v_y * w_x, v_x * scalar_field, v_y * scalar_field, v_z * scalar_field], axis=1)


def project_outputs(spectra, waves):
    k_x, k_y, k_z, k_sq, keep_mask = waves
    spectra = jnp.where(keep_mask, spectra, 0.0)
    n_x, n_y, n_z = spectra[:, 0], spectra[:, 1], spectra[:, 2]
    k_dot = (k_x * n_x + k_y * n_y + k_z * n_z) / jnp.where(k_sq > 0, k_sq, 1.0)
    vel_rhs = jnp.stack([n_x - k_x * k_dot, n_y - k_y * k_dot, n_z - k_z * k_dot], axis=1)
    scal_rhs = -1j * (k_x * spectra[:, 3] + k_y * spectra[:, 4] + k_z * spectra[:, 5])
    return jnp.real(vel_rhs), jnp.imag(vel_rhs), jnp.real(scal_rhs), jnp.imag(scal_rhs)


def exchange(spectra, axis_name, split_axis, concat_axis):
    wire_pair = jnp.stack([jnp.real(spectra), jnp.imag(spectra)])
    wire_pair = lax.all_to_all(wire_pair, axis_name, split_axis + 1, concat_axis + 1, tiled=True)
    return lax.complex(wire_pair[0], wire_pair[1])


def solution(mesh):
    spec_vec = P('ens', None, None, 'row', 'col')
    spec_scal = P('ens', None, 'row', 'col')

    def local_term(vel_re, vel_im, scal_re, scal_im):
        grid_n = vel_re.shape[2]
        y_count = vel_re.shape[3]
        z_count = vel_re.shape[4]
        waves = wave_numbers(grid_n, lax.axis_index('row') * y_count, y_count, lax.axis_index('col') * z_count, z_count)
        spectra = spectral_fields(lax.complex(vel_re, vel_im), lax.complex(scal_re, scal_im), waves)
        spectra = jnp.fft.ifft(spectra, axis=2, norm='ortho')
        spectra = exchange(spectra, 'row', 2, 3)
        spectra = jnp.fft.ifft(spectra, axis=3, norm='ortho')
        spectra = exchange(spectra, 'col', 3, 4)
        physical = jnp.fft.irfft(spectra, n=grid_n, axis=4, norm='ortho')
        spectra = jnp.fft.rfft(grid_products(physical), axis=4, norm='ortho')[..., : grid_n // 2]
        spectra = exchange(spectra, 'col', 4, 3)
        spectra = jnp.fft.fft(spectra, axis=3, norm='ortho')
        spectra = exchange(spectra, 'row', 3, 2)
        spectra = jnp.fft.fft(spectra, axis=2, norm='ortho')
        return project_outputs(spectra, waves)

    return jax.shard_map(local_term, mesh=mesh, in_specs=(spec_vec, spec_vec, spec_scal, spec_scal), out_specs=(spec_vec, spec_vec, spec_scal, spec_scal), check_vma=False)
```

profile of v0, /device:TPU:1, one launch (start us, length us, event | category | flops | bytes accessed | tf_op | source)
XLA Modules:
  0.0 1075.6 jit_solution(442880044012172144)
XLA Ops:
  1.7 8.3 fusion.173
  15.2 9.1 fusion.16
  27.8 8.7 fusion.18
  36.5 17.0 %fusion.15 = (f32[1,64,7,32,8,8]{1,3,5,4,2,0:T(8,128)}, f32[1,64,7,32,8,8]{1,3,5,4,2,0:T(8,128)}) fusion(f32[]{:T(128)S(6)} %multiply.518, f32[]{:T(128)S(6)} %multiply.516, f32[64,7,8,8,32]{0,4,3,2,1:T(8,128)} %fusion.18, f32[32,64,7,8,8]{1,0,4,3,2:T(8,128)} %fusion.16, f32[64,7,32,8,8]{0,2,4,3,1:T(8,128)} %copy-done.2), kind=kOutput, calls=%fused_computation.37 | convolution fusion | flops 363336704 | bytes 18350088 | tf_op jit(solution)/shard_map/jit(fft)/dot.16 | solution.py:67
  53.5 13.9 %pad_maximum_fusion = f32[2,64,7,32,8,8]{1,3,5,4,2,0:T(8,128)} fusion(f32[1,64,7,32,8,8]{1,3,5,4,2,0:T(8,128)} %get-tuple-element.114, f32[1,64,7,32,8,8]{1,3,5,4,2,0:T(8,128)} %get-tuple-element.113), kind=kLoop, calls=%fused_computation.3 | loop fusion | flops 1835008 | bytes 14680064 | tf_op jit(solution)/shard_map/stack | solution.py:52
  67.4 18.8 %copy.94 = f32[2,64,7,32,8,8]{1,5,4,2,0,3:T(8,128)} copy(f32[2,64,7,32,8,8]{1,3,5,4,2,0:T(8,128)} %pad_maximum_fusion) | data formatting | bytes 14680064 | tf_op jit(solution)/shard_map/stack | solution.py:52
  86.2 13.1 %reshape.230 = f32[4,1,458752]{2,1,0:T(1,128)} reshape(f32[32,2,7,8,8,64]{5,4,3,2,1,0:T(8,128)} %bitcast.319) | data formatting | bytes 14680064
  99.3 88.5 %all_to_all.56 = f32[4,1,458752]{2,1,0:T(1,128)} all-to-all(f32[4,1,458752]{2,1,0:T(1,128)} %reshape.230), channel_id=1, replica_groups=mesh['ens'=1,'col'=2,'row'=4] {'row'}, dimensions={0} | all-to-all | bytes 14680064 | tf_op jit(solution)/shard_map/all_to_all | solution.py:53
  188.3 24.1 %reduce.6 = f32[4,458752]{1,0:T(4,128)} reduce(f32[4,1,458752]{2,1,0:T(1,128)} %all_to_all.56, f32[]{:T(128)} %broadcast.1143), dimensions={1}, to_apply=%all_to_all.40.reduce_sub_computation | reduce | bytes 14680068 | tf_op jit(solution)/shard_map/all_to_all | solution.py:53
  212.4 15.0 %reshape.231 = f32[32,2,7,8,8,64]{5,4,3,2,1,0:T(8,128)} reshape(f32[4,458752]{1,0:T(4,128)} %reduce.6) | data formatting | bytes 14680064
  227.3 13.8 %copy.90 = f32[2,64,7,4,8,8,8]{1,5,3,6,4,2,0:T(8,128)} copy(f32[2,64,7,4,8,8,8]{1,6,5,2,0,4,3:T(8,128)} %bitcast.320) | data formatting | bytes 14680064 | tf_op jit(solution)/shard_map/all_to_all | solution.py:53
  241.1 12.5 %fusion.22 = f32[64,7,8,8,32]{0,4,3,2,1:T(8,128)} fusion(f32[2,64,7,8,4,8,8]{1,5,4,6,3,2,0:T(8,128)} %bitcast.312), kind=kOutput, calls=%fused_computation.49 | convolution fusion | flops 353243136 | bytes 11010048 | tf_op jit(solution)/shard_map/jit(fft)/dot | solution.py:69
  253.6 8.9 fusion.24
  262.5 16.1 %fusion.13 = (f32[1,64,7,8,32,8]{1,4,5,3,2,0:T(8,128)}, f32[1,64,7,8,32,8]{1,4,5,3,2,0:T(8,128)}) fusion(f32[]{:T(128)S(6)} %multiply.518, f32[]{:T(128)S(6)} %multiply.516, f32[64,7,8,8,32]{0,4,3,2,1:T(8,128)} %fusion.22, f32[32,64,7,8,8]{1,0,4,3,2:T(8,128)} %fusion.24, f32[2,64,7,8,4,8,8]{1,5,4,6,3,2,0:T(8,128)S(1)} %bitcast.314), kind=kOutput, calls=%fused_computation.31 | convolution fusion | flops 363336704 | bytes 22020104 | tf_op jit(solution)/shard_map/jit(fft)/dot.15 | solution.py:69
  278.7 13.9 %pad_maximum_fusion.1 = f32[2,64,7,8,32,8]{1,4,5,3,2,0:T(8,128)} fusion(f32[1,64,7,8,32,8]{1,4,5,3,2,0:T(8,128)} %get-tuple-element.112, f32[1,64,7,8,32,8]{1,4,5,3,2,0:T(8,128)} %get-tuple-element.111), kind=kLoop, calls=%fused_computation.4 | loop fusion | flops 1835008 | bytes 14680064 | tf_op jit(solution)/shard_map/stack | solution.py:52
  292.6 18.8 %copy.93 = f32[2,64,7,8,32,8]{1,5,3,2,0,4:T(8,128)} copy(f32[2,64,7,8,32,8]{1,4,5,3,2,0:T(8,128)} %pad_maximum_fusion.1) | data formatting | bytes 14680064 | tf_op jit(solution)/shard_map/stack | solution.py:52
  311.4 19.2 %reshape.232 = f32[2,1,917504]{2,1,0:T(1,128)} reshape(f32[32,2,7,8,8,64]{5,4,3,2,1,0:T(8,128)} %bitcast.321) | data formatting | bytes 14680064
  330.6 6.6 all-to-all-start.1
  337.2 7.7 fusion.30
  344.9 73.1 %all-to-all-done.1 = f32[2,1,917504]{2,1,0:T(1,128)} async-done(((f32[2,1,917504]{2,1,0:T(1,128)}), f32[2,1,917504]{2,1,0:T(1,128)}, u32[]{:S(2)}, u32[]{:S(2)}) %all-to-all-start.1) | async-done | bytes 7340064 | tf_op jit(solution)/shard_map/all_to_all | solution.py:53
  418.0 26.8 %reduce.7 = f32[2,917504]{1,0:T(2,128)} reduce(f32[2,1,917504]{2,1,0:T(1,128)} %all-to-all-done.1, f32[]{:T(128)} %broadcast.1143), dimensions={1}, to_apply=%all_to_all.43.reduce_sub_computation | reduce | bytes 14680068 | tf_op jit(solution)/shard_map/all_to_all | solution.py:53
  444.8 16.1 %reshape.233 = f32[32,2,7,8,8,64]{5,4,3,2,1,0:T(8,128)} reshape(f32[2,917504]{1,0:T(2,128)} %reduce.7) | data formatting | bytes 14680064
  460.9 12.4 %copy.89 = f32[2,64,7,8,2,16,8]{1,6,4,5,3,2,0:T(8,128)} copy(f32[2,64,7,8,2,16,8]{1,6,3,2,0,5,4:T(8,128)} %bitcast.322) | data formatting | bytes 14680064 | tf_op jit(solution)/shard_map/all_to_all | solution.py:53
  473.3 12.3 %slice_bitcast_fusion.1 = (f32[64,7,8,16,16]{0,4,3,2,1:T(8,128)}, f32[64,7,8,16,16]{0,4,3,2,1:T(8,128)}) fusion(f32[2,64,7,8,16,2,8]{1,6,5,4,3,2,0:T(8,128)} %bitcast.318), kind=kLoop, calls=%fused_computation.25 | loop fusion | bytes 14680064 | tf_op jit(solution)/shard_map/squeeze | solution.py:54
  485.6 7.4 jit_fft_.332
  493.0 12.1 %jit_fft_.139 = f32[64,7,8,16,15]{0,4,3,2,1:T(8,128)} reverse(f32[64,7,8,16,15]{0,4,3,2,1:T(8,128)} %jit_fft_.332), dimensions={4} | reverse | bytes 6881280 | tf_op jit(solution)/shard_map/jit(fft) | solution.py:71
  505.2 20.3 %fusion.4 = f32[64,7,8,16,32]{0,4,3,2,1:T(8,128)} fusion(f32[64,7,8,16,16]{0,4,3,2,1:T(8,128)} %get-tuple-element.121, f32[64,7,8,16,15]{0,4,3,2,1:T(8,128)} %jit_fft_.139), kind=kOutput, calls=%fused_computation.14 | convolution fusion | flops 710153216 | bytes 14450688 | tf_op jit(solution)/shard_map/jit(fft) | solution.py:71
  525.5 3.7 jit_fft_.333
  529.2 12.1 %jit_fft_.142 = f32[64,7,8,16,15]{0,4,3,2,1:T(8,128)} reverse(f32[64,7,8,16,15]{0,4,3,2,1:T(8,128)} %jit_fft_.333), dimensions={4} | reverse | bytes 6881280 | tf_op jit(solution)/shard_map/jit(fft) | solution.py:71
  541.4 7.0 jit_fft_.286
  548.4 19.4 %fusion.5 = f32[64,7,8,16,32]{0,4,3,2,1:T(8,128)} fusion(f32[64,7,8,16,16]{0,4,3,2,1:T(8,128)S(1)} %bitcast.339, f32[64,7,8,16,15]{0,4,3,2,1:T(8,128)} %jit_fft_.286), kind=kOutput, calls=%fused_computation.15 | convolution fusion | flops 710153216 | bytes 14450688 | tf_op jit(solution)/shard_map/jit(fft) | solution.py:71
  567.8 29.1 %add_multiply_fusion = f32[64,7,8,16,32]{0,4,3,2,1:T(8,128)} fusion(f32[64,7,8,16,32]{0,4,3,2,1:T(8,128)} %fusion.5, f32[64,7,8,16,32]{0,4,3,2,1:T(8,128)} %fusion.4, f32[64,7,8,16,16]{0,4,3,2,1:T(8,128)} %get-tuple-element.121, f32[64,7,8,16,15]{0,4,3,2,1:T(8,128)} %jit_fft_.139, f32[64,7,8,16,16]{0,4,3,2,1:T(8,128)} %get-tuple-element.122, ...), kind=kOutput, calls=%fused_computation.7 | convolution fusion | flops 724832256 | bytes 36241408 | tf_op jit(solution)/shard_map/jit(fft) | solution.py:71
  597.0 4.7 subtract_dynamic-update-slice_fusion.2
  601.6 4.7 subtract_dynamic-update-slice_fusion.1
  606.3 4.7 subtract_dynamic-update-slice_fusion
  619.5 11.3 %fusion.41 = f32[64,6,8,16,32]{0,4,3,2,1:T(8,128)S(1)} fusion(f32[64,6,8,16,32]{0,4,3,2,1:T(8,128)S(1)} %multiply_dynamic-update-slice_fusion), kind=kOutput, calls=%fused_computation.124 | convolution fusion | flops 603983872 | bytes 12582912 | tf_op jit(solution)/shard_map/jit(fft) | solution.py:72
  630.8 13.4 %fusion.55 = f32[64,6,8,16,32]{0,4,3,2,1:T(8,128)} fusion(f32[64,6,8,16,32]{0,4,3,2,1:T(8,128)S(1)} %multiply_dynamic-update-slice_fusion), kind=kOutput, calls=%fused_computation.138 | convolution fusion | flops 603984896 | bytes 12582912 | tf_op jit(solution)/shard_map/jit(fft) | solution.py:72
  644.2 11.7 %slice_subtract_fusion = (f32[64,6,8,16,17]{0,4,3,2,1:T(8,128)S(1)}, f32[64,6,8,16,17]{0,4,3,2,1:T(8,128)}) fusion(f32[64,6,8,16,32]{0,4,3,2,1:T(8,128)} %fusion.30, f32[64,6,8,16,32]{0,4,3,2,1:T(8,128)S(1)} %fusion.41, f32[64,6,8,16,32]{0,4,3,2,1:T(8,128)} %fusion.55), kind=kLoop, calls=%fused_computation.17 | loop fusion | flops 1671168 | bytes 16711680 | tf_op jit(solution)/shard_map/jit(fft) | solution.py:72
  655.9 5.5 subtract_bitcast_fusion.1
  661.4 9.2 pad_maximum_fusion.2
  670.5 13.2 %copy.96 = f32[2,64,6,8,16,16]{1,4,3,2,0,5:T(8,128)} copy(f32[2,64,6,8,16,16]{1,5,4,3,2,0:T(8,128)} %pad_maximum_fusion.2) | data formatting | bytes 12582912 | tf_op jit(solution)/shard_map/stack | solution.py:52
  683.7 16.7 %reshape.234 = f32[2,1,786432]{2,1,0:T(1,128)} reshape(f32[16,2,6,8,16,64]{5,4,3,2,1,0:T(8,128)} %bitcast.330) | data formatting | bytes 12582912
  700.4 77.5 %all_to_all.57 = f32[2,1,786432]{2,1,0:T(1,128)} all-to-all(f32[2,1,786432]{2,1,0:T(1,128)} %reshape.234), channel_id=1, replica_groups=mesh['ens'=1,'col'=2,'row'=4] {'col'}, dimensions={0} | all-to-all | bytes 12582912 | tf_op jit(solution)/shard_map/all_to_all | solution.py:53
  777.9 23.2 %reduce.8 = f32[2,786432]{1,0:T(2,128)} reduce(f32[2,1,786432]{2,1,0:T(1,128)} %all_to_all.57, f32[]{:T(128)} %broadcast.1143), dimensions={1}, to_apply=%all_to_all.46.reduce_sub_computation | reduce | bytes 12582916 | tf_op jit(solution)/shard_map/all_to_all | solution.py:53
  801.1 14.1 %reshape.235 = f32[16,2,6,8,16,64]{5,4,3,2,1,0:T(8,128)} reshape(f32[2,786432]{1,0:T(2,128)} %reduce.8) | data formatting | bytes 12582912
  815.2 11.1 %copy.92 = f32[2,64,6,8,16,2,8]{1,4,5,6,3,2,0:T(8,128)} copy(f32[2,64,6,8,16,2,8]{1,4,3,2,0,6,5:T(8,128)} %bitcast.331) | data formatting | bytes 12582912 | tf_op jit(solution)/shard_map/all_to_all | solution.py:53
  826.3 9.4 fusion.172
  835.7 6.5 fusion.53
  842.2 7.8 fusion.28
  850.0 11.6 %subtract_bitcast_fusion = (f32[1,64,6,8,32,8]{1,4,5,3,2,0:T(8,128)S(1)}, f32[1,64,6,8,32,8]{1,4,5,3,2,0:T(8,128)}) fusion(f32[64,6,8,8,32]{0,4,3,2,1:T(8,128)} %fusion.28, f32[64,6,8,8,32]{0,4,3,2,1:T(8,128)S(1)} %fusion.53, f32[64,6,8,8,32]{0,4,3,2,1:T(8,128)S(1)} %bitcast.328), kind=kOutput, calls=%fused_computation.62 | convolution fusion | flops 308286464 | bytes 15728640 | tf_op jit(solution)/shard_map/jit(fft) | solution.py:74
  861.6 9.6 pad_maximum_fusion.3
  871.2 16.4 %copy.95 = f32[2,64,6,8,32,8]{1,5,3,2,0,4:T(8,128)} copy(f32[2,64,6,8,32,8]{1,4,5,3,2,0:T(8,128)} %pad_maximum_fusion.3) | data formatting | bytes 12582912 | tf_op jit(solution)/shard_map/stack | solution.py:52
  887.5 11.5 %reshape.236 = f32[4,1,393216]{2,1,0:T(1,128)} reshape(f32[32,2,6,8,8,64]{5,4,3,2,1,0:T(8,128)} %bitcast.332) | data formatting | bytes 12582912
  899.1 7.8 all-to-all-start.3
  907.3 69.1 %all-to-all-done.3 = f32[4,1,393216]{2,1,0:T(1,128)} async-done(((f32[4,1,393216]{2,1,0:T(1,128)}), f32[4,1,393216]{2,1,0:T(1,128)}, u32[]{:S(2)}, u32[]{:S(2)}) %all-to-all-start.3) | async-done | bytes 6291488 | tf_op jit(solution)/shard_map/all_to_all | solution.py:53
  976.4 20.9 %reduce.9 = f32[4,393216]{1,0:T(4,128)} reduce(f32[4,1,393216]{2,1,0:T(1,128)} %all-to-all-done.3, f32[]{:T(128)} %broadcast.1143), dimensions={1}, to_apply=%all_to_all.49.reduce_sub_computation | reduce | bytes 12582916 | tf_op jit(solution)/shard_map/all_to_all | solution.py:53
  997.3 13.0 %reshape.237 = f32[32,2,6,8,8,64]{5,4,3,2,1,0:T(8,128)} reshape(f32[4,393216]{1,0:T(4,128)} %reduce.9) | data formatting | bytes 12582912
  1010.3 12.0 %copy.91 = f32[2,64,6,8,4,8,8]{1,3,4,6,5,2,0:T(8,128)} copy(f32[2,64,6,8,4,8,8]{1,6,3,2,0,5,4:T(8,128)} %bitcast.333) | data formatting | bytes 12582912 | tf_op jit(solution)/shard_map/all_to_all | solution.py:53
  1022.3 10.1 fusion.32
  1032.4 7.5 fusion.33
  1039.9 13.7 %bitcast_select_fusion.1 = (f32[64,6,32,8,8]{0,2,4,3,1:T(8,128)}, f32[64,6,32,8,8]{0,2,4,3,1:T(8,128)}) fusion(pred[32,8,8]{0,2,1:T(8,128)(4,1)S(1)} %get-tuple-element.141, f32[64,6,8,8,32]{0,4,3,2,1:T(8,128)} %fusion.32, f32[64,6,8,8,32]{0,4,3,2,1:T(8,128)} %fusion.33, f32[2,64,6,4,8,8,8]{1,4,3,6,5,2,0:T(8,128)S(1)} %bitcast.317), kind=kOutput, calls=%fused_computation.58 | convolution fusion | flops 310644736 | bytes 18876416 | tf_op jit(solution)/shard_map/jit(fft) | solution.py:76
  1053.6 4.0 multiply_add_fusion.4
  1067.7 3.5 copy.60
  1071.7 3.5 copy.59
  (81 shorter events, 29.5 us)
Async XLA Ops:
  0.6 12.5 %copy-start.7 = (f32[32]{0:T(128)}, f32[32]{0:T(128)S(1)}, u32[]{:S(2)}) copy-start(f32[32]{0:T(128)S(1)} %convert_multiply_fusion.4) | copy-start | bytes 388
  1.2 11.2 %copy-start.9 = (f32[8]{0:T(128)}, f32[8]{0:T(128)S(1)}, u32[]{:S(2)}) copy-start(f32[8]{0:T(128)S(1)} %get-tuple-element.144) | copy-start | bytes 100
  1.7 11.5 %copy-start.11 = (f32[8]{0:T(128)}, f32[8]{0:T(128)S(1)}, u32[]{:S(2)}) copy-start(f32[8]{0:T(128)S(1)} %get-tuple-element.146) | copy-start | bytes 100
  10.0 2.5 copy-start.4
  13.2 1.4 copy-start.5
  15.2 9.1 copy-start.6
  24.9 2.9 copy-start.2
  241.1 12.5 %copy-start = (f32[2,64,7,4,8,8,8]{1,5,3,6,4,2,0:T(8,128)S(1)}, f32[2,64,7,4,8,8,8]{1,5,3,6,4,2,0:T(8,128)}, u32[]{:S(2)}) copy-start(f32[2,64,7,4,8,8,8]{1,5,3,6,4,2,0:T(8,128)} %copy.90) | copy-start | bytes 22020100
  330.6 87.4 %all-to-all-start.1 = ((f32[2,1,917504]{2,1,0:T(1,128)}), f32[2,1,917504]{2,1,0:T(1,128)}, u32[]{:S(2)}, u32[]{:S(2)}) async-start(f32[2,1,917504]{2,1,0:T(1,128)} %reshape.232), calls=%async_computation.1 | async-start | bytes 14680064 | tf_op jit(solution)/shard_map/all_to_all | solution.py:53
  493.0 32.5 %slice-start.4 = ((s8[7340032]{0:T(1024)(128)(4,1)}), s8[3145728]{0:T(1024)(128)(4,1)S(1)}, s32[]{:S(2)}) async-start(s8[7340032]{0:T(1024)(128)(4,1)} %bitcast.336), calls=%async_computation.8 | async-start | bytes 6291456
  505.1 20.3 %slice-start.5 = ((s8[7340032]{0:T(1024)(128)(4,1)}), s8[4194304]{0:T(1024)(128)(4,1)S(1)}, s32[]{:S(2)}) async-start(s8[7340032]{0:T(1024)(128)(4,1)} %bitcast.336), calls=%async_computation.9 | async-start | bytes 8388608
  529.2 19.2 %slice-start.6 = ((s8[7340032]{0:T(1024)(128)(4,1)}), s8[3145728]{0:T(1024)(128)(4,1)S(1)}, s32[]{:S(2)}) async-start(s8[7340032]{0:T(1024)(128)(4,1)} %bitcast.338), calls=%async_computation.10 | async-start | bytes 6291456
  541.4 7.0 slice-start.7
  835.7 6.5 slice-start
  835.7 6.5 slice-start.1
  899.1 7.9 copy-start.14
  899.1 8.0 copy-start.13
  899.1 77.3 %all-to-all-start.3 = ((f32[4,1,393216]{2,1,0:T(1,128)}), f32[4,1,393216]{2,1,0:T(1,128)}, u32[]{:S(2)}, u32[]{:S(2)}) async-start(f32[4,1,393216]{2,1,0:T(1,128)} %reshape.236), calls=%async_computation.3 | async-start | bytes 12582912 | tf_op jit(solution)/shard_map/all_to_all | solution.py:53
  1022.3 10.1 copy-start.1
  1039.9 13.7 %copy-start.8 = (f32[32]{0:T(128)S(1)}, f32[32]{0:T(128)}, u32[]{:S(2)}) copy-start(f32[32]{0:T(128)} %copy-done.7) | copy-start | bytes 388
  1039.9 13.7 %copy-start.10 = (f32[8]{0:T(128)S(1)}, f32[8]{0:T(128)}, u32[]{:S(2)}) copy-start(f32[8]{0:T(128)} %copy-done.9) | copy-start | bytes 100
  1039.9 13.7 %copy-start.12 = (f32[8]{0:T(128)S(1)}, f32[8]{0:T(128)}, u32[]{:S(2)}) copy-start(f32[8]{0:T(128)} %copy-done.11) | copy-start | bytes 100
  1053.6 4.7 copy-start.3
  1061.0 4.7 slice-start.2
  1062.8 2.9 slice-start.3
where the time goes:
time: 1080 us
  local copies, waits for them, and re-layouts  316 us (29%)
  matrix products  231 us (21%)
  other arithmetic  205 us (19%)
  blocking collectives  166 us (15%)
  waiting for transfers between devices  142 us (13%)
  starting transfers between devices  14.4 us (1%)
    all_to_all x2, blocking collectives, exchange(): lax.all_to_all(wire_pair, axis_name, split_axis + 1, concat_axis + 1, til...  166 us
    all_to_all x2, waiting for transfers between devices, exchange(): lax.all_to_all(wire_pair, axis_name, split_axis + 1, concat_axis + 1, til...  142 us
    unnamed x59, local copies, waits for them, and re-layouts  141 us
    all_to_all x4, other arithmetic, exchange(): lax.all_to_all(wire_pair, axis_name, split_axis + 1, concat_axis + 1, til...  95 us
    another operation x3, matrix products, local_term(): physical = jnp.fft.irfft(spectra, n=grid_n, axis=4, norm='ortho')  68.8 us
    another operation x4, local copies, waits for them, and re-layouts, exchange(): wire_pair = jnp.stack([jnp.real(spectra), jnp.imag(spectra)])  67.2 us
    another operation x5, other arithmetic, exchange(): wire_pair = jnp.stack([jnp.real(spectra), jnp.imag(spectra)])  52 us
    all_to_all x5, local copies, waits for them, and re-layouts, exchange(): lax.all_to_all(wire_pair, axis_name, split_axis + 1, concat_axis + 1, til...  49.8 us
  transfers between devices with their start and end apart: 2, of which 2 were waited for; matrix products, arithmetic and copies ran while one was open for 1% of the time, Pallas kernels for 0%

commit v1 on v0

v1 whole, which is shorter than its diff:
```python
import math

import jax
import jax.numpy as jnp
import numpy as np
from jax import lax
from jax.experimental import pallas as pl
from jax.experimental.pallas import tpu as pltpu
from jax.sharding import PartitionSpec as P

N = 32
LANES = 128
FLOWS = 64
ROWS = 2048
TILE = (8, LANES)
D_TILES, S_TILES = 24, 12
K = 256
COLS = 512
TINY = 1e-9
MIB = 1 << 20
PAIR, VEC, FIELDS, PEERS = range(2), range(3), range(4), range(1, 8)
MESH = pl.DeviceIdType.MESH
F32 = jnp.float32
BF16 = jnp.bfloat16
SLOTS = list(range(S_TILES)) + list(range(20, 32))
OWNERS = [("D", 0, 0, 0), ("D", 0, 3, 32), ("S", 0, 1, FLOWS), ("S", 0, 2, 68),
          ("D", 1, 0, 84), ("D", 1, 3, 86), ("S", 1, 1, 116), ("S", 1, 2, 110)]

FIRST = [0, 32, FLOWS, 76]


def mode(j):
    return j if j < N // 2 else j - N


def kept(m):
    return 3 * abs(m) < N


def lane_owner(lane):
    if lane < OWNERS[4][3]:
        return sum(lane >= first for first in FIRST[1:4])
    base = 4 if lane < OWNERS[6][3] else 6
    return base + (lane % 4) // 2


def lane_mode(lane, parity):
    own = lane_owner(lane)
    kind, col, row, start = OWNERS[own]
    off = lane - start
    ky_local, kz_half = off // 4, off % 4
    if row == 2:
        ky_local += 4
    if own == 7 and ky_local > 7:
        return None
    ky = mode(8 * row + ky_local)
    kz = 8 * col + 2 * kz_half + parity
    if not (kept(ky) and kept(kz)):
        return None
    return ky, kz


def split3(x):
    x = np.asarray(x, np.float32)
    hi = x.astype(BF16)
    rest = x - hi.astype(np.float32)
    mid = rest.astype(BF16)
    low = (rest - mid.astype(np.float32)).astype(BF16)
    return np.stack([hi, mid, low])


def tables():
    scale = float(N) ** -1.5
    inv = np.zeros((2, K, COLS))
    fwd = np.zeros((2, COLS, K))
    ky_t = np.zeros((2, LANES))
    kz_t = np.zeros((2, LANES))
    yy, zz = np.meshgrid(np.arange(N), np.arange(N // 2), indexing="ij")
    for parity in PAIR:
        for lane in range(LANES):
            got = lane_mode(lane, parity)
            if got is None:
                continue
            ky, kz = got
            ang = 2 * np.pi * ((ky * yy + kz * zz) % N).reshape(-1) / N
            weight = 1.0 if kz == 0 else 2.0
            inv[parity, lane] = weight * scale * np.cos(ang)
            inv[parity, LANES + lane] = -weight * scale * np.sin(ang)
            fwd[parity, :, lane] = scale * np.cos(ang)
            fwd[parity, :, LANES + lane] = -scale * np.sin(ang)
            ky_t[parity, lane] = ky
            kz_t[parity, lane] = kz
    unit = 2 * np.pi / N
    inv3 = np.stack([split3(inv[p]) for p in PAIR])
    fwd3 = np.stack([split3(fwd[p]) for p in PAIR])
    wave = np.zeros((2, 2, 8, LANES), np.float32)
    wave[:, 0] = (ky_t * unit)[:, None]
    wave[:, 1] = (kz_t * unit)[:, None]
    kx = np.array([mode(j) for j in SLOTS]) * unit
    k_sq = kx[None, :, None] ** 2 + ((ky_t * unit) ** 2 + (kz_t * unit) ** 2)[:, None]
    ok = (k_sq > 0) & np.array([kept(mode(j)) for j in SLOTS])[None, :, None]
    inv_sq = np.where(ok, 1.0 / np.where(k_sq > 0, k_sq, 1.0), 0.0)
    proj = np.zeros((2, D_TILES, 2, 8, LANES), np.float32)
    proj[:, :, 0] = inv_sq[:, :, None]
    proj[:, :, 1] = ok[:, :, None]
    return inv3, fwd3, wave, proj


def cmul_const(a, c, s):
    re, im = a
    if abs(s) < TINY:
        return (re, im) if c > 0 else (-re, -im)
    if abs(c) < TINY:
        return (-im, re) if s > 0 else (im, -re)
    if abs(abs(c) - abs(s)) < TINY:
        r = abs(c)
        sc, ss = (1 if c > 0 else -1), (1 if s > 0 else -1)
        p, q = (re - im) * r, (re + im) * r
        if sc > 0 and ss > 0:
            return p, q
        if sc > 0:
            return q, -p
        if ss > 0:
            return -q, p
        return -p, -q
    return re * c - im * s, re * s + im * c


def fft(vals, sign):
    n = len(vals)
    if n == 1:
        return list(vals)
    even, odd = fft(vals[0::2], sign), fft(vals[1::2], sign)
    out = [None] * n
    for k in range(n // 2):
        a, b = even[k], odd[k]
        if b is not None:
            ang = sign * 2 * math.pi * k / n
            b = cmul_const(b, math.cos(ang), math.sin(ang))
        if a is None and b is None:
            continue
        if b is None:
            out[k], out[k + n // 2] = a, a
        elif a is None:
            out[k], out[k + n // 2] = b, (-b[0], -b[1])
        else:
            out[k] = (a[0] + b[0], a[1] + b[1])
            out[k + n // 2] = (a[0] - b[0], a[1] - b[1])
    return out


def dot(a, b):
    return jnp.dot(a, b, preferred_element_type=F32)


def split_bf16(x):
    hi = x.astype(BF16)
    rest = x - hi.astype(F32)
    mid = rest.astype(BF16)
    low = (rest - mid.astype(F32)).astype(BF16)
    return hi, mid, low


def dev_of(row, col):
    return col * 4 + row


def slot_of(row, col):
    return col * 2 + (1 if row >= 2 else 0)


def six_products(parts, table):
    hi, mid, low = parts
    t_hi, t_mid, t_low = (table[p] for p in VEC)
    acc = dot(low, t_hi) + dot(hi, t_low) + dot(mid, t_mid)
    return acc + dot(mid, t_hi) + dot(hi, t_mid) + dot(hi, t_hi)


def main_kernel(vre, vim, sre, sim, inv_hbm, fwd_hbm, wave, proj, back,
                xin, send, recv_d, recv_s, merged, lhs, phys, prod, spec, res, ret_d, ret_s,
                inv, fwd, in_sem, tab_sem, s1, r1, s2, r2):
    row, col, ens = lax.axis_index("row"), lax.axis_index("col"), lax.axis_index("ens")
    me = dev_of(row, col)
    dense = jnp.logical_or(row == 0, row == 3)
    sparse = jnp.logical_not(dense)
    my_slot = col * 2 + jnp.where(row >= 2, 1, 0)

    loads = []
    for f in FIELDS:
        for ri in PAIR:
            src = (vre, vim)[ri].at[f] if f < 3 else (sre, sim)[ri].at[0]
            for half in PAIR:
                cp = pltpu.make_async_copy(
                    src.at[pl.ds(1280 * half, 768)], xin.at[f, ri, pl.ds(768 * half, 768)], in_sem.at[f, ri, half])
                cp.start()
                loads.append(cp)
    tab = [pltpu.make_async_copy(inv_hbm, inv, tab_sem.at[0]), pltpu.make_async_copy(fwd_hbm, fwd, tab_sem.at[1])]
    for cp in tab:
        cp.start()

    barrier = pltpu.get_barrier_semaphore()

    def peer(k):
        return row ^ (k % 4), col ^ (k // 4)

    for k in PEERS:
        pr, pc = peer(k)
        pl.semaphore_signal(barrier, inc=1, device_id=(ens, pc, pr), device_id_type=MESH)
    pl.semaphore_wait(barrier, 7)

    def pack_dense(f):
        def body(t, carry):
            ri, rest = t // S_TILES, t % S_TILES
            b, q = rest // 6, rest % 6
            blk = xin[f, ri, pl.ds(q * K + b, LANES, stride=2), :]
            send[:, f, t] = blk.T.reshape(8, *TILE)
            return carry
        lax.fori_loop(0, D_TILES, body, 0, unroll=2)

    def pack_sparse(f):
        first = jnp.where(row == 1, 0, 32)

        def body(t, carry):
            ri, rest = t // 6, t % 6
            b, g = rest // 3, rest % 3
            parts = [xin[f, ri, pl.ds(g * COLS + s * FLOWS + first + b, 16, stride=2), :] for s in range(8)]
            send[:, f, t] = jnp.concatenate(parts, axis=0).T.reshape(8, *TILE)
            return carry
        lax.fori_loop(0, S_TILES, body, 0, unroll=2)

    def first_copy(kind, f, pr, pc):
        to = dev_of(pr, pc)
        if kind == "D":
            src, dst = send.at[to, f], recv_d.at[my_slot, f]
        else:
            src, dst = send.at[to, f, pl.ds(0, S_TILES)], recv_s.at[my_slot, f]
        return pltpu.make_async_remote_copy(
            src_ref=src, dst_ref=dst, send_sem=s1.at[to, f], recv_sem=r1.at[me, f],
            device_id=(ens, pc, pr), device_id_type=MESH)

    for f in FIELDS:
        for cp in loads[4 * f:4 * f + 4]:
            cp.wait()

        @pl.when(dense)
        def _():
            pack_dense(f)
            for k in PEERS:
                first_copy("D", f, *peer(k)).start()
            recv_d[my_slot, f] = send[me, f]

        @pl.when(sparse)
        def _():
            pack_sparse(f)
            for k in PEERS:
                first_copy("S", f, *peer(k)).start()
            recv_s[my_slot, f] = send[me, f, 0:S_TILES]

    lane = lax.broadcasted_iota(jnp.int32, TILE, 1)
    low = lane % 4 < 2
    edges = FIRST + [OWNERS[4][3], OWNERS[6][3], LANES]
    spans = [(lane >= lo) & (lane < hi) for lo, hi in zip(edges[:-1], edges[1:])]
    owned = spans[:4] + [spans[4] & low, spans[4] & ~low, spans[5] & low, spans[5] & ~low]

    def wait_field(f):
        for kind, c, r, _ in OWNERS:
            d = dev_of(r, c)
            slot = slot_of(r, c)

            @pl.when(me != d)
            def _():
                if kind == "D":
                    src, dst = send.at[d, f], recv_d.at[slot, f]
                else:
                    src, dst = send.at[d, f, pl.ds(0, S_TILES)], recv_s.at[slot, f]
                pltpu.make_async_remote_copy(
                    src_ref=src, dst_ref=dst, send_sem=s1.at[d, f], recv_sem=r1.at[d, f],
                    device_id=(ens, c, r), device_id_type=MESH).wait_recv()

    def merge(f):
        def body(t, carry):
            rb, g = t // 3, t % 3
            for s8 in range(8):
                q, s = 2 * g + s8 // 4, s8 % 4
                acc = None
                for o, (kind, c, r, start) in enumerate(OWNERS):
                    slot = slot_of(r, c)
                    if kind == "D":
                        tile, shift = recv_d[slot, f, rb * 6 + q], (start - 32 * s) % LANES
                    else:
                        tile, shift = recv_s[slot, f, rb * 3 + g], (start - 16 * s8) % LANES
                    if shift:
                        tile = pltpu.roll(tile, shift, 1)
                    acc = tile if acc is None else jnp.where(owned[o], tile, acc)
                merged[f, rb, 8 * g + s8] = acc
            return carry
        lax.fori_loop(0, S_TILES, body, 0)

    def to_x(f, b, get):
        vals = [None] * N
        for i, j in enumerate(SLOTS):
            if kept(mode(j)):
                vals[j] = get(i)
        out = fft(vals, 1)
        for x in range(0, N, 2):
            for ri in PAIR:
                pair = jnp.concatenate([out[x][ri], out[x + 1][ri]], axis=0)
                for p, part in enumerate(split_bf16(pair)):
                    lhs[f, b, 8 * x:8 * x + 16, K * p + LANES * ri:K * p + LANES * ri + LANES] = part

    def field_x(f, src):
        def body(b, carry):
            to_x(f, b, lambda i: (merged[src, b, i], merged[src, 2 + b, i]))
            return carry
        lax.fori_loop(0, 2, body, 0)

    def curl_x(f):
        c1, c2 = (f + 1) % 3, (f + 2) % 3

        def body(b, carry):
            ky, kz = wave[b, 0], wave[b, 1]

            def get(i):
                kx = 2 * math.pi * mode(SLOTS[i]) / N
                ks = (kx, ky, kz)
                im = ks[c1] * merged[c2, b, i] - ks[c2] * merged[c1, b, i]
                re = ks[c2] * merged[c1, 2 + b, i] - ks[c1] * merged[c2, 2 + b, i]
                return re, im
            to_x(3 + f, b, get)
            return carry
        lax.fori_loop(0, 2, body, 0)

    def to_grid(f):
        halves = []
        for b in PAIR:
            halves.append(six_products([lhs[f, b, :, K * p:K * p + K] for p in VEC], inv.at[b]))
        phys[f, 0] = halves[0] + halves[1]
        phys[f, 1] = halves[0] - halves[1]

    def to_spec(c):
        for b in PAIR:
            spec[c, b] = six_products([prod[b, p] for p in VEC], fwd.at[b])

    def fold(rows, n0, n1):
        for b, v in enumerate((n0 + n1, n0 - n1)):
            for p, part in enumerate(split_bf16(v)):
                prod[b, p, rows, :] = part

    def cross(c):
        c1, c2 = (c + 1) % 3, (c + 2) % 3

        def body(i, carry):
            rows = pl.ds(pl.multiple_of(i * 16, 16), 16)
            n = [phys[c1, h, rows, :] * phys[3 + c2, h, rows, :] - phys[c2, h, rows, :] * phys[3 + c1, h, rows, :]
                 for h in PAIR]
            fold(rows, *n)
            return carry
        lax.fori_loop(0, 16, body, 0)
        to_spec(c)

    def flux(c):
        def body(i, carry):
            rows = pl.ds(pl.multiple_of(i * 16, 16), 16)
            fold(rows, *[phys[c, h, rows, :] * phys[6, h, rows, :] for h in PAIR])
            return carry
        lax.fori_loop(0, 16, body, 0)
        to_spec(c)

    def from_x(c):
        def body(b, carry):
            vals = [(spec[c, b, 8 * x:8 * x + 8, 0:LANES], spec[c, b, 8 * x:8 * x + 8, LANES:K]) for x in range(N)]
            out = fft(vals, -1)
            for i, j in enumerate(SLOTS):
                merged[c, b, i] = out[j][0]
                merged[c, 2 + b, i] = out[j][1]
            return carry
        lax.fori_loop(0, 2, body, 0)

    unit = 2 * math.pi / N

    def kx_of(i):
        j = jnp.where(i < S_TILES, i, i - D_TILES)
        return j.astype(F32) * unit

    def project():
        def body(t, carry):
            b, i = t // D_TILES, t % D_TILES
            ks = (kx_of(i), wave[b, 0], wave[b, 1])
            inv_sq, ok = proj[b, i, 0], proj[b, i, 1]
            for ri in PAIR:
                n = [merged[c, 2 * ri + b, i] for c in VEC]
                kd = (ks[0] * n[0] + ks[1] * n[1] + ks[2] * n[2]) * inv_sq
                for c in VEC:
                    res[c, 2 * ri + b, i] = (n[c] - ks[c] * kd) * ok
            return carry
        lax.fori_loop(0, 48, body, 0, unroll=4)

    def diverge():
        def body(t, carry):
            b, i = t // D_TILES, t % D_TILES
            ks = (kx_of(i), wave[b, 0], wave[b, 1])
            ok = proj[b, i, 1]
            sums = [ks[0] * merged[0, 2 * ri + b, i] + ks[1] * merged[1, 2 * ri + b, i] + ks[2] * merged[2, 2 * ri + b, i]
                    for ri in PAIR]
            res[3, b, i] = sums[1] * ok
            res[3, 2 + b, i] = -sums[0] * ok
            return carry
        lax.fori_loop(0, 48, body, 0, unroll=4)

    def unmerge(f):
        zero = jnp.zeros(TILE, F32)

        def body(t, carry):
            rb, g = t // 3, t % 3
            for o, (kind, c, r, start) in enumerate(OWNERS):
                slot = slot_of(r, c)
                width = 32 if kind == "D" else 16
                valid = None
                if kind == "S":
                    valid = lane % 16 < S_TILES if r == 1 else lane % 16 >= 8
                if c == 1:
                    valid = low if valid is None else valid & low
                for part in range(2 if kind == "D" else 1):
                    acc = None
                    for s in range(LANES // width):
                        i = 8 * g + 4 * part + s
                        tile = res[f, rb, i]
                        shift = (width * s - start) % LANES
                        if shift:
                            tile = pltpu.roll(tile, shift, 1)
                        acc = tile if acc is None else jnp.where(lane // width == s, tile, acc)
                    if valid is not None:
                        acc = jnp.where(valid, acc, zero)
                    if kind == "D":
                        ret_d[slot, f, rb * 6 + 2 * g + part] = acc
                    else:
                        ret_s[slot, f, rb * 3 + g] = acc
            return carry
        lax.fori_loop(0, S_TILES, body, 0)

    def second_copy(kind, f, r, c):
        slot = slot_of(r, c)
        if kind == "D":
            src, dst = ret_d.at[slot, f], back.at[me, f]
        else:
            src, dst = ret_s.at[slot, f], back.at[me, f, pl.ds(0, S_TILES)]
        d = dev_of(r, c)
        return pltpu.make_async_remote_copy(
            src_ref=src, dst_ref=dst, send_sem=s2.at[d, f], recv_sem=r2.at[me, f],
            device_id=(ens, c, r), device_id_type=MESH)

    def arrival(kind, k, f):
        pr, pc = peer(k)
        d = dev_of(pr, pc)
        if kind == "D":
            src, dst = ret_d.at[0, f], back.at[d, f]
        else:
            src, dst = ret_s.at[0, f], back.at[d, f, pl.ds(0, S_TILES)]
        return pltpu.make_async_remote_copy(
            src_ref=src, dst_ref=dst, send_sem=s2.at[d, f], recv_sem=r2.at[d, f],
            device_id=(ens, pc, pr), device_id_type=MESH)

    def send_back(f):
        for kind, c, r, _ in OWNERS:
            d = dev_of(r, c)

            @pl.when(me != d)
            def _():
                second_copy(kind, f, r, c).start()

            @pl.when(me == d)
            def _():
                slot = slot_of(r, c)
                if kind == "D":
                    back[d, f] = ret_d[slot, f]
                else:
                    back[d, f, 0:S_TILES] = ret_s[slot, f]

    for f in VEC:
        wait_field(f)
        merge(f)
        field_x(f, f)
    for f in VEC:
        curl_x(f)
    tab[0].wait()
    lax.fori_loop(0, 6, lambda f, carry: (to_grid(f), carry)[1], 0)
    tab[1].wait()
    for c in VEC:
        cross(c)
        from_x(c)
    project()
    for f in VEC:
        unmerge(f)
        send_back(f)
    wait_field(3)
    merge(3)
    field_x(6, 3)
    to_grid(6)
    for c in VEC:
        flux(c)
        from_x(c)
    diverge()
    unmerge(3)
    send_back(3)

    for kind, mine in (("D", dense), ("S", sparse)):
        @pl.when(mine)
        def _():
            for k in PEERS:
                for f in FIELDS:
                    first_copy(kind, f, *peer(k)).wait_send()
                    arrival(kind, k, f).wait_recv()

    for kind, c, r, _ in OWNERS:
        @pl.when(me != dev_of(r, c))
        def _():
            for f in FIELDS:
                second_copy(kind, f, r, c).wait_send()


def out_kernel(back, ore, oim, tre, tim, buf, sem):
    row = lax.axis_index("row")
    dense = jnp.logical_or(row == 0, row == 3)
    copies = []
    for f in FIELDS:
        for ri in PAIR:
            dst = (ore, oim)[ri].at[f] if f < 3 else (tre, tim)[ri].at[0]
            copies.append(pltpu.make_async_copy(buf.at[f, ri], dst, sem.at[f, ri]))
    for f in FIELDS:
        for ri in PAIR:
            buf[f, ri, 768:1280, :] = jnp.zeros((COLS, FLOWS), F32)

            @pl.when(dense)
            def _():
                def body(t, carry):
                    b, q = t // 6, t % 6
                    tile = back[:, f, ri * S_TILES + t].reshape(FLOWS, LANES).T
                    base = q * K + jnp.where(q >= 3, COLS, 0)
                    buf[f, ri, pl.ds(base + b, LANES, stride=2), :] = tile
                    return carry
                lax.fori_loop(0, S_TILES, body, 0, unroll=2)

            @pl.when(jnp.logical_not(dense))
            def _():
                buf[f, ri, 0:768, :] = jnp.zeros((768, FLOWS), F32)
                buf[f, ri, 1280:ROWS, :] = jnp.zeros((768, FLOWS), F32)
                first = jnp.where(row == 1, 0, 32)

                def body(t, carry):
                    b, g = t // 3, t % 3
                    tile = back[:, f, ri * 6 + t].reshape(FLOWS, LANES).T
                    for s in range(8):
                        i = g * 8 + s
                        j = i + jnp.where(i >= S_TILES, 8, 0)
                        buf[f, ri, pl.ds(j * FLOWS + first + b, 16, stride=2), :] = tile[16 * s:16 * s + 16]
                    return carry
                lax.fori_loop(0, 6, body, 0)

            copies[2 * f + ri].start()
    for cp in copies:
        cp.wait()


def solution(mesh):
    spec_vec = P('ens', None, None, 'row', 'col')
    spec_scal = P('ens', None, 'row', 'col')
    inv_np, fwd_np, wave_np, proj_np = tables()

    def local_term(vel_re, vel_im, scal_re, scal_im):
        vec = [jnp.transpose(a, (1, 2, 3, 4, 0)).reshape(3, ROWS, FLOWS) for a in (vel_re, vel_im)]
        scal = [jnp.transpose(a, (1, 2, 3, 0)).reshape(1, ROWS, FLOWS) for a in (scal_re, scal_im)]
        vmem = pl.BlockSpec(memory_space=pltpu.VMEM)
        hbm = pl.BlockSpec(memory_space=pl.ANY)
        dma = pltpu.SemaphoreType.DMA
        links = dma((8, 4))
        all_tiles = (8, 4, D_TILES, *TILE)
        d_buf = pltpu.VMEM((4, 4, D_TILES, *TILE), F32)
        s_buf = pltpu.VMEM((4, 4, S_TILES, *TILE), F32)
        inv_buf = pltpu.VMEM(inv_np.shape, BF16)
        back = pl.pallas_call(
            main_kernel,
            out_shape=jax.ShapeDtypeStruct(all_tiles, F32),
            in_specs=[hbm] * 6 + [vmem] * 2,
            out_specs=vmem,
            scratch_shapes=[
                pltpu.VMEM((4, 2, 1536, FLOWS), F32), pltpu.VMEM(all_tiles, F32), d_buf, s_buf, d_buf,
                pltpu.VMEM((7, 2, K, 3 * K), BF16), pltpu.VMEM((7, 2, K, COLS), F32), inv_buf,
                pltpu.VMEM((3, 2, K, K), F32), d_buf, d_buf, s_buf, inv_buf, pltpu.VMEM(fwd_np.shape, BF16),
                dma((4, 2, 2)), dma((2,)), links, links, links, links,
            ],
            compiler_params=pltpu.CompilerParams(
                collective_id=0, has_side_effects=True, vmem_limit_bytes=60 * MIB),
            name="flow_home",
        )(*vec, *scal, jnp.asarray(inv_np), jnp.asarray(fwd_np), jnp.asarray(wave_np), jnp.asarray(proj_np))
        outs = pl.pallas_call(
            out_kernel,
            out_shape=[jax.ShapeDtypeStruct((3, ROWS, FLOWS), F32)] * 2 + [jax.ShapeDtypeStruct((1, ROWS, FLOWS), F32)] * 2,
            in_specs=[vmem],
            out_specs=[hbm] * 4,
            scratch_shapes=[pltpu.VMEM((4, 2, ROWS, FLOWS), F32), pltpu.SemaphoreType.DMA((4, 2))],
            compiler_params=pltpu.CompilerParams(vmem_limit_bytes=40 * MIB),
            name="lay_out",
        )(back)
        out_v = [jnp.transpose(a.reshape(3, N, 8, 8, FLOWS), (4, 0, 1, 2, 3)) for a in outs[:2]]
        out_s = [jnp.transpose(a.reshape(N, 8, 8, FLOWS), (3, 0, 1, 2)) for a in outs[2:]]
        return (*out_v, *out_s)

    return jax.shard_map(local_term, mesh=mesh, in_specs=(spec_vec, spec_vec, spec_scal, spec_scal),
                         out_specs=(spec_vec, spec_vec, spec_scal, spec_scal), check_vma=False)
```

time: 1080 us -> 83 us (0.08)
  local copies, waits for them, and re-layouts: 316 us -> 1.88 us
  matrix products: 231 us -> 0 us
  other arithmetic: 205 us -> 0 us
  blocking collectives: 166 us -> 0 us
  waiting for transfers between devices: 142 us -> 0 us
  Pallas kernels: 0 us -> 79.9 us
  starting transfers between devices: 14.4 us -> 0 us
    another operation x18 -> x0, matrix products: 231 us -> none  [the longest x3 68.8 us: local_term(): physical = jnp.fft.irfft(spectra, n=grid_n, axis=4, norm='ortho')]
    all_to_all x2 -> x0, blocking collectives: 166 us -> none  [exchange(): lax.all_to_all(wire_pair, axis_name, split_axis + 1, concat_axis + 1, til...]
    all_to_all x2 -> x0, waiting for transfers between devices: 142 us -> none  [exchange(): lax.all_to_all(wire_pair, axis_name, split_axis + 1, concat_axis + 1, til...]
    unnamed x59 -> x2, local copies, waits for them, and re-layouts: 141 us -> 1.88 us
    another operation x10 -> x0, local copies, waits for them, and re-layouts: 104 us -> none  [the longest x4 67.2 us: exchange(): wire_pair = jnp.stack([jnp.real(spectra), jnp.imag(spectra)])]
    all_to_all x4 -> x0, other arithmetic: 95 us -> none  [exchange(): lax.all_to_all(wire_pair, axis_name, split_axis + 1, concat_axis + 1, til...]
    pallas_call x0 -> x2, Pallas kernels: none -> 79.9 us  [the longest x1 73.5 us: local_term(): pl.pallas_call(main_kernel, out_shape=jax.ShapeDtypeStruct(all_tiles, F32...]
    another operation x10 -> x0, other arithmetic: 74.6 us -> none  [the longest x5 52 us: exchange(): wire_pair = jnp.stack([jnp.real(spectra), jnp.imag(spectra)])]
  transfers between devices with their start and end apart: 2 -> 0, of which waited for: 2 -> 0; matrix products, arithmetic and copies ran while one was open for 1% -> 0% of each run, Pallas kernels for 0% -> 0%
where the time goes in v1:
time: 83 us; the launch traced here: 82.4 us
  Pallas kernels  79.9 us (96%)
  local copies, waits for them, and re-layouts  1.88 us (2%)
    pallas_call x1, Pallas kernels, local_term(): pl.pallas_call(main_kernel, out_shape=jax.ShapeDtypeStruct(all_tiles, F32...  73.5 us
    pallas_call x1, Pallas kernels, local_term(): pl.pallas_call(out_kernel, out_shape=[jax.ShapeDtypeStruct((3, ROWS, FLOW...  6.39 us
    unnamed x2, local copies, waits for them, and re-layouts  1.88 us

profile of v1, /device:TPU:1, one launch (start us, length us, event | category | flops | bytes accessed | tf_op | source)
XLA Modules:
  0.0 82.4 jit_solution(10582688882167578596)
XLA Ops:
  0.6 73.5 %flow_home.1.back = f32[8,4,24,8,128]{4,3,2,1,0:T(8,128)} custom-call(f32[3,2048,64]{2,1,0:T(8,128)} %bitcast.24, f32[3,2048,64]{2,1,0:T(8,128)} %bitcast.25, f32[1,2048,64]{2,1,0:T(8,128)} %bitcast.26, f32[1,2048,64]{2,1,0:T(8,128)} %bitcast.27, bf16[2,3,256,512]{3,2,1,0:T(8,128)(2,1)} %constant.8.clone.inv_hbm, ...), custom_call_target="tpu_custom_call" | custom-call | tf_op jit(solution)/shard_map/flow_home/pallas_call | solution.py:580
  74.1 0.0 copy-start
  74.1 1.9 %copy-done = f32[8,4,24,8,128]{4,3,2,1,0:T(8,128)S(1)} copy-done((f32[8,4,24,8,128]{4,3,2,1,0:T(8,128)S(1)}, f32[8,4,24,8,128]{4,3,2,1,0:T(8,128)}, u32[]{:S(2)}) %copy-start) | copy-done | bytes 3145752
  76.0 6.4 %lay_out.1 = (f32[3,2048,64]{2,1,0:T(8,128)}, f32[3,2048,64]{2,1,0:T(8,128)}, f32[1,2048,64]{2,1,0:T(8,128)}, f32[1,2048,64]{2,1,0:T(8,128)}) custom-call(f32[8,4,24,8,128]{4,3,2,1,0:T(8,128)S(1)} %copy-done), custom_call_target="tpu_custom_call" | custom-call | tf_op jit(solution)/shard_map/lay_out/pallas_call | solution.py:595
Async XLA Ops:
  74.1 1.9 %copy-start = (f32[8,4,24,8,128]{4,3,2,1,0:T(8,128)S(1)}, f32[8,4,24,8,128]{4,3,2,1,0:T(8,128)}, u32[]{:S(2)}) copy-start(f32[8,4,24,8,128]{4,3,2,1,0:T(8,128)} %flow_home.1.back) | copy-start | bytes 9437188

commit v2 on v0

v2 whole, which is shorter than its diff:
```python
import math

import jax
import jax.numpy as jnp
import numpy as np
from jax import lax
from jax.experimental import pallas as pl
from jax.experimental.pallas import tpu as pltpu
from jax.sharding import PartitionSpec as P

N = 32
LANES = 128
FLOWS = 64
ROWS = 2048
TILE = (8, LANES)
K = 256
TINY = 1e-9
MIB = 1 << 20
QUAD, OCT, HALF = 4, 8, 16
PAIR, VEC, FIELDS, PEERS = range(2), range(3), range(QUAD), range(1, OCT)
MESH = pl.DeviceIdType.MESH
F32 = jnp.float32
BF16 = jnp.bfloat16
UNIT = 2 * math.pi / N
SLOTS = list(range(11)) + list(range(22, N))
KEPT = len(SLOTS)
KEPT_ROWS = KEPT * FLOWS
LOW_ROWS = 11 * FLOWS
D_OUT, S_OUT, D_RET, S_RET = 21, 11, HALF, OCT
D_CHUNKS, S_CHUNKS = (0, 6, 11, HALF, 21), (0, 3, 6, OCT, 11)
RET_CHUNKS = (0, QUAD, 10, HALF)
DENSE = [(0, 0), (3, 0), (0, 1), (3, 1)]
SPARSE = [(1, 0), (2, 0), (1, 1), (2, 1)]


def mode(j):
    return j if j < N // 2 else j - N


def kept(m):
    return 3 * abs(m) < N


def home_mode(lane, parity):
    block, p = divmod(lane, N)
    y, high, half = p // QUAD, p % QUAD // 2, p % QUAD
    if block < 2:
        row, col = 3 * block, 0
    elif block == 2:
        row, col, half = 3 * high, 1, p % 2
    elif p < 12:
        row, col = 1, 0
    elif p < 20:
        row, col, y = 2, 0, y + 3
    else:
        row, col, half, y = 1 + high, 1, p % 2, y - 5 + 6 * high
    if y > 7:
        return None
    ky, kz = mode(OCT * row + y), OCT * col + 2 * half + parity
    return (ky, kz) if kept(ky) and kept(kz) else None


def source_mode(lane, row, col, parity):
    width = N if row % 3 == 0 else HALF
    block, p = divmod(lane, width)
    slot = block if width == N else block // 2 + QUAD * (block % 2)
    y = p // QUAD + (QUAD if row == 2 else 0)
    ky, kz = mode(OCT * row + y), OCT * col + 2 * (p % QUAD) + parity
    return slot, ((ky, kz) if kept(ky) and kept(kz) else None)


def basis(kx, ky, kz):
    flat, full = math.hypot(kx, ky), math.hypot(kx, ky, kz)
    if full == 0:
        return np.zeros(3), np.zeros(3)
    if flat == 0:
        return np.array([1.0, 0, 0]), np.array([0, 1.0, 0])
    e1 = np.array([ky, -kx, 0]) / flat
    return e1, np.array([kx * kz, ky * kz, -flat * flat]) / (flat * full)


def split3(x):
    x = np.asarray(x, np.float32)
    hi = x.astype(BF16)
    rest = x - hi.astype(np.float32)
    mid = rest.astype(BF16)
    return hi, mid, (rest - mid.astype(np.float32)).astype(BF16)


def tables():
    scale = float(N) ** -1.5
    half = N // 2
    points = [(y, z) for z in range(1, OCT) for y in range(N)] + [(y, z) for z in (0, OCT) for y in range(half)]
    yy, zz = np.array(points).T
    inv = np.zeros((2, 2, LANES, K))
    wave = np.zeros((2, QUAD, LANES), np.float32)
    home = np.zeros((2, KEPT, 5, LANES), np.float32)
    for parity in PAIR:
        for lane in range(LANES):
            got = home_mode(lane, parity)
            if got is None:
                continue
            ky, kz = got
            ang = UNIT * (ky * (yy + 0.5) + kz * zz)
            inv[parity, 0, lane] = scale * np.cos(ang)
            inv[parity, 1, lane] = -scale * np.sin(ang)
            wave[parity, :, lane] = ky * UNIT, kz * UNIT, math.cos(UNIT * ky / 2), math.sin(UNIT * ky / 2)
            for i, j in enumerate(SLOTS):
                e1, e2 = basis(mode(j), ky, kz)
                home[parity, i, :, lane] = *e1[:2], *e2
    fwd = np.swapaxes(inv, 2, 3)
    weight = np.full((2, 1, LANES, 1), 2.0)
    for lane in range(LANES):
        got = home_mode(lane, 0)
        if got is not None and got[1] == 0:
            weight[0, 0, lane] = 1.0
    hi, mid, low = split3(inv * weight)
    inv3 = np.stack([np.concatenate(pair, axis=2) for pair in ((hi, low), (mid, mid), (hi, hi))], axis=2)
    fwd3 = np.concatenate(split3(fwd), axis=3)
    return inv3, fwd3, wave, home.reshape(-1, LANES)


def source_tables():
    out = np.zeros((OCT, 2, S_OUT, 3, LANES), np.float32)
    for row in FIELDS:
        for col in PAIR:
            per = QUAD if row % 3 == 0 else OCT
            for parity in PAIR:
                for lane in range(LANES):
                    slot, got = source_mode(lane, row, col, parity)
                    for t in range(S_OUT):
                        n = t * per + slot
                        i = n // 2
                        if n >= 2 * KEPT:
                            out[dev_of(row, col), parity, t, 0, lane] = 1.0
                        elif got is not None:
                            e1, e2 = basis(mode(SLOTS[i]), *got)
                            out[dev_of(row, col), parity, t, :, lane] = (e2[1], e1[1], e2[2]) if n % 2 else (e1[0], e2[0], 0)
    return out.reshape(OCT, -1, LANES)


def cmul_const(a, c, s):
    re, im = a
    if abs(s) < TINY:
        return (re, im) if c > 0 else (-re, -im)
    if abs(c) < TINY:
        return (-im, re) if s > 0 else (im, -re)
    if abs(abs(c) - abs(s)) < TINY:
        p, q = (re - im) * abs(c), (re + im) * abs(c)
        if c > 0:
            return (p, q) if s > 0 else (q, -p)
        return (-q, p) if s > 0 else (-p, -q)
    return re * c - im * s, re * s + im * c


def fft(vals, sign):
    n = len(vals)
    if n == 1:
        return list(vals)
    even, odd = fft(vals[0::2], sign), fft(vals[1::2], sign)
    out = [None] * n
    for k in range(n // 2):
        a, b = even[k], odd[k]
        if b is not None:
            ang = sign * 2 * math.pi * k / n
            b = cmul_const(b, math.cos(ang), math.sin(ang))
        if a is None and b is None:
            continue
        if b is None:
            out[k], out[k + n // 2] = a, a
        elif a is None:
            out[k], out[k + n // 2] = b, (-b[0], -b[1])
        else:
            out[k] = (a[0] + b[0], a[1] + b[1])
            out[k + n // 2] = (a[0] - b[0], a[1] - b[1])
    return out


def dot(a, b):
    return jnp.dot(a, b, preferred_element_type=F32)


def split_bf16(x):
    hi = x.astype(BF16)
    rest = x - hi.astype(F32)
    mid = rest.astype(BF16)
    low = (rest - mid.astype(F32)).astype(BF16)
    return hi, mid, low


def dev_of(row, col):
    return col * QUAD + row


def roll(x, shift):
    return pltpu.roll(x, shift % LANES, 1)


def main_kernel(vre, vim, sre, sim, inv_hbm, fwd_hbm, wave_hbm, home_hbm, back,
                xin, send, recv_d, recv_s, merged, lhs, phys, prod, spec, bins, res, ret_d, ret_s,
                inv, fwd, wave, home, in_sem, tab_sem, s1, r1, s2, r2):
    row, col, ens = lax.axis_index("row"), lax.axis_index("col"), lax.axis_index("ens")
    me = dev_of(row, col)
    dense = jnp.logical_or(row == 0, row == 3)
    sparse = jnp.logical_not(dense)
    my_slot = col * 2 + jnp.where(row >= 2, 1, 0)

    loads = []
    for f in FIELDS:
        for ri in PAIR:
            src = (vre, vim)[ri].at[f] if f < 3 else (sre, sim)[ri].at[0]
            for half, (a, size, b) in enumerate(((0, LOW_ROWS, 0), (2 * LOW_ROWS, KEPT_ROWS - LOW_ROWS, LOW_ROWS))):
                cp = pltpu.make_async_copy(
                    src.at[pl.ds(a, size)], xin.at[ri, pl.ds(KEPT_ROWS * f + b, size)], in_sem.at[f, ri, half])
                cp.start()
                loads.append(cp)
    tab = [pltpu.make_async_copy(src, dst, tab_sem.at[i]) for i, (src, dst) in enumerate(
        ((wave_hbm, wave), (inv_hbm, inv), (fwd_hbm, fwd), (home_hbm, home)))]
    for cp in tab:
        cp.start()

    barrier = pltpu.get_barrier_semaphore()

    def peer(k):
        return row ^ (k % QUAD), col ^ (k // QUAD)

    for k in PEERS:
        pr, pc = peer(k)
        pl.semaphore_signal(barrier, inc=1, device_id=(ens, pc, pr), device_id_type=MESH)
    for ri in PAIR:
        xin[ri, QUAD * KEPT_ROWS:, :] = jnp.zeros((QUAD * FLOWS, FLOWS), F32)
    pl.semaphore_wait(barrier, 7)

    def pack_dense(lo, hi):
        def body(n, carry):
            t, rb = n // QUAD, n % QUAD
            blk = xin[rb // 2, pl.ds(t * K + rb % 2, LANES, stride=2), :]
            send[:, t, rb] = blk.T.reshape(OCT, *TILE)
            return carry
        lax.fori_loop(QUAD * lo, QUAD * hi, body, 0, unroll=QUAD)

    def pack_sparse(lo, hi):
        first = jnp.where(row == 1, 0, N)

        def body(n, carry):
            t, rb = n // QUAD, n % QUAD
            base = t * OCT * FLOWS + first + rb % 2
            parts = [xin[rb // 2, pl.ds(base + (p // 2 + QUAD * (p % 2)) * FLOWS, HALF, stride=2), :] for p in range(OCT)]
            send[:, t, rb] = jnp.concatenate(parts, axis=0).T.reshape(OCT, *TILE)
            return carry
        lax.fori_loop(QUAD * lo, QUAD * hi, body, 0, unroll=QUAD)

    def remote(src, dst, sems, i, j, chunk, r, c):
        return pltpu.make_async_remote_copy(
            src_ref=src, dst_ref=dst, send_sem=sems[0].at[i, chunk], recv_sem=sems[1].at[j, chunk],
            device_id=(ens, c, r), device_id_type=MESH)

    def bounds(kind, chunk):
        edges = D_CHUNKS if kind == "D" else S_CHUNKS
        return edges[chunk], edges[chunk + 1]

    def out_copy(kind, chunk, slot, r, c, frm):
        lo, hi = bounds(kind, chunk)
        to = dev_of(r, c)
        part = pl.ds(lo, hi - lo)
        dst = recv_d if kind == "D" else recv_s
        return remote(send.at[to, part], dst.at[slot, part], (s1, r1), to, frm, chunk, r, c)

    for chunk in FIELDS:
        for cp in loads[QUAD * chunk + (QUAD if chunk else 0):QUAD * chunk + OCT]:
            cp.wait()

        for kind, mine, pack, recv in (("D", dense, pack_dense, recv_d), ("S", sparse, pack_sparse, recv_s)):
            @pl.when(mine)
            def _():
                lo, hi = bounds(kind, chunk)
                pack(lo, hi)
                for k in PEERS:
                    out_copy(kind, chunk, my_slot, *peer(k), me).start()
                recv[my_slot, lo:hi] = send[me, lo:hi]

    lane = lax.broadcasted_iota(jnp.int32, TILE, 1)
    low = lane % QUAD < 2
    p32 = lane % N
    left, even, first_half = lane < FLOWS, lane % FLOWS < N, p32 < HALF

    def everyone():
        for kind, group in (("D", DENSE), ("S", SPARSE)):
            for slot, (r, c) in enumerate(group):
                yield kind, slot, r, c

    def wait_chunk(chunk):
        for kind, slot, r, c in everyone():
            @pl.when(me != dev_of(r, c))
            def _():
                out_copy(kind, chunk, slot, r, c, dev_of(r, c)).wait_recv()

    def swap_blocks(tiles, forward):
        def outer(a, b, c, d):
            return (jnp.where(left, a, roll(c, FLOWS)), jnp.where(left, b, roll(d, FLOWS)),
                    jnp.where(left, roll(a, FLOWS), c), jnp.where(left, roll(b, FLOWS), d))

        def inner(a, b, c, d):
            return (jnp.where(even, a, roll(b, N)), jnp.where(even, roll(a, -N), b),
                    jnp.where(even, c, roll(d, N)), jnp.where(even, roll(c, -N), d))
        return inner(*outer(*tiles)) if forward else outer(*inner(*tiles))

    def merge(lo, hi):
        def body(b, carry):
            cos, sin = wave[b, pl.ds(2, 1)], wave[b, pl.ds(3, 1)]
            for t in range(lo, hi):
                got = []
                for ri in PAIR:
                    rb = 2 * ri + b
                    d = [recv_d[o, t, rb] for o in FIELDS]
                    s = [recv_s[o, t // 2, rb] for o in FIELDS]
                    h = HALF * (t % 2)
                    c1 = jnp.where(low, d[2], roll(d[3], 2))
                    s0 = roll(s[0], -h) if h else s[0]
                    rest = jnp.where(low, roll(s[2], 20 - h), roll(s[3], 14 - h))
                    s1_ = jnp.where(p32 < 12, s0, jnp.where(p32 < 20, roll(s[1], QUAD - h), rest))
                    got.append(swap_blocks((d[0], d[1], c1, s1_), True))
                for s, (re, im) in enumerate(zip(*got)):
                    merged[b, QUAD * t + s] = re * cos + im * sin
                    merged[2 + b, QUAD * t + s] = im * cos - re * sin
            return carry
        lax.fori_loop(0, 2, body, 0)

    def to_x(f, b, get):
        vals = [None] * N
        for i, j in enumerate(SLOTS):
            vals[j] = get(i)
        out = fft(vals, 1)
        for x in range(0, N, 2):
            for ri in PAIR:
                hi, mid, lo = split_bf16(jnp.concatenate([out[x][ri], out[x + 1][ri]], axis=0))
                for p, part in enumerate((lo, hi, mid)):
                    lhs[f, b, ri, OCT * x:OCT * x + HALF, LANES * p:LANES * p + LANES] = part

    def field_x(f, src):
        def body(b, carry):
            to_x(f, b, lambda i: (merged[b, src * KEPT + i], merged[2 + b, src * KEPT + i]))
            return carry
        lax.fori_loop(0, 2, body, 0)

    def curl_x(f):
        c1, c2 = (f + 1) % 3, (f + 2) % 3

        def body(b, carry):
            ky, kz = (jnp.broadcast_to(wave[b, pl.ds(i, 1)], TILE) for i in PAIR)

            def get(i):
                ks = (UNIT * mode(SLOTS[i]), ky, kz)
                m1, m2 = c1 * KEPT + i, c2 * KEPT + i
                im = ks[c1] * merged[b, m2] - ks[c2] * merged[b, m1]
                re = ks[c2] * merged[2 + b, m1] - ks[c1] * merged[2 + b, m2]
                return re, im
            to_x(3 + f, b, get)
            return carry
        lax.fori_loop(0, 2, body, 0)

    def to_grid(f):
        sums = []
        for b in PAIR:
            parts = []
            for ri in PAIR:
                low_hi, hi_mid = lhs[f, b, ri, :, 0:K], lhs[f, b, ri, :, LANES:LANES + K]
                acc = dot(low_hi, inv[b, ri, 0]) + dot(hi_mid, inv[b, ri, 1])
                parts.append(acc + dot(hi_mid, inv[b, ri, 2]))
            sums.append((parts[0] + parts[1], parts[0] - parts[1]))
        for side in PAIR:
            phys[f, 2 * side] = sums[0][side] + sums[1][side]
            phys[f, 2 * side + 1] = sums[0][side] - sums[1][side]

    def to_spec(c):
        for b in PAIR:
            for ri in PAIR:
                hi, mid, lo = (prod[b, ri, p] for p in VEC)
                both = dot(hi, fwd[b, ri, :, 0:K]) + dot(mid, fwd[b, ri, :, 0:K])
                small = dot(lo, fwd[b, ri, :, 0:LANES]) + dot(hi, fwd[b, ri, :, K:])
                spec[c, b, ri] = small + both[:, LANES:] + both[:, :LANES]

    def product(c, point):
        def body(i, carry):
            rows = pl.ds(pl.multiple_of(i * HALF, HALF), HALF)
            n = [point(q, rows) for q in FIELDS]
            for b in PAIR:
                side = [n[0] - n[1], n[2] - n[3]] if b else [n[0] + n[1], n[2] + n[3]]
                for ri in PAIR:
                    v = side[0] - side[1] if ri else side[0] + side[1]
                    for p, part in enumerate(split_bf16(v)):
                        prod[b, ri, p, rows, :] = part
            return carry
        lax.fori_loop(0, HALF, body, 0, unroll=2)
        to_spec(c)

    def cross(c):
        c1, c2 = (c + 1) % 3, (c + 2) % 3
        product(c, lambda q, rows: phys[c1, q, rows, :] * phys[3 + c2, q, rows, :]
                - phys[c2, q, rows, :] * phys[3 + c1, q, rows, :])

    def flux(c):
        product(c, lambda q, rows: phys[c, q, rows, :] * phys[6, q, rows, :])

    def from_x(c):
        def body(b, carry):
            vals = [tuple(spec[c, b, ri, OCT * x:OCT * x + OCT, :] for ri in PAIR) for x in range(N)]
            out = fft(vals, -1)
            for i, j in enumerate(SLOTS):
                for ri in PAIR:
                    bins[c, 2 * ri + b, i] = out[j][ri]
            return carry
        lax.fori_loop(0, 2, body, 0)

    def phase(b, re, im):
        cos, sin = wave[b, pl.ds(2, 1)], wave[b, pl.ds(3, 1)]
        return re * cos - im * sin, re * sin + im * cos

    def project():
        def body(t, carry):
            b, i = t // KEPT, t % KEPT
            e = [home[pl.ds(t * 5 + k, 1)] for k in range(5)]
            n = [[bins[c, 2 * ri + b, i] for c in VEC] for ri in PAIR]
            one = [e[0] * n[ri][0] + e[1] * n[ri][1] for ri in PAIR]
            two = [e[2] * n[ri][0] + e[3] * n[ri][1] + e[QUAD] * n[ri][2] for ri in PAIR]
            for which, v in enumerate((one, two)):
                for ri, part in enumerate(phase(b, *v)):
                    res[2 * ri + b, 2 * i + which] = part
            return carry
        lax.fori_loop(0, 2 * KEPT, body, 0, unroll=6)

    def diverge():
        def body(b, carry):
            for i, j in enumerate(SLOTS):
                ks = (UNIT * mode(j), wave[b, pl.ds(0, 1)], wave[b, pl.ds(1, 1)])
                re, im = phase(b, *[sum(ks[c] * bins[c, 2 * ri + b, i] for c in VEC) for ri in PAIR])
                res[b, 2 * KEPT + i] = im
                res[2 + b, 2 * KEPT + i] = -re
            for ri in PAIR:
                res[2 * ri + b, 3 * KEPT] = jnp.zeros(TILE, F32)
            return carry
        lax.fori_loop(0, 2, body, 0)

    def unmerge(lo, hi):
        p16 = lane % HALF
        zero = jnp.zeros(TILE, F32)

        def body(rb, carry):
            for t in range(lo, hi, 2):
                ends = []
                for h in PAIR:
                    tiles = swap_blocks([res[rb, QUAD * (t + h) + s] for s in FIELDS], False)
                    ret_d[0, t + h, rb], ret_d[1, t + h, rb] = tiles[:2]
                    ret_d[2, t + h, rb] = jnp.where(low, tiles[2], zero)
                    ret_d[3, t + h, rb] = jnp.where(low, roll(tiles[2], -2), zero)
                    ends.append(tiles[3])
                for o, (a, ok) in enumerate(((0, p16 < 12), (-QUAD, p16 >= OCT), (-20, (p16 < 12) & low), (-14, (p16 >= OCT) & low))):
                    v = jnp.where(first_half, roll(ends[0], a) if a else ends[0], roll(ends[1], a + HALF))
                    ret_s[o, t // 2, rb] = jnp.where(ok, v, zero)
            return carry
        lax.fori_loop(0, QUAD, body, 0)

    def ret_copy(kind, chunk, slot, r, c, frm):
        lo, hi = RET_CHUNKS[chunk], RET_CHUNKS[chunk + 1]
        if kind == "S":
            lo, hi = lo // 2, hi // 2
        part = pl.ds(lo, hi - lo)
        src = ret_d if kind == "D" else ret_s
        return remote(src.at[slot, part], back.at[frm, part], (s2, r2), dev_of(r, c), frm, chunk, r, c)

    def send_back(chunk):
        for kind, slot, r, c in everyone():
            d = dev_of(r, c)

            @pl.when(me != d)
            def _():
                ret_copy(kind, chunk, slot, r, c, me).start()

            @pl.when(me == d)
            def _():
                lo, hi = RET_CHUNKS[chunk], RET_CHUNKS[chunk + 1]
                if kind == "D":
                    back[d, lo:hi] = ret_d[slot, lo:hi]
                else:
                    back[d, lo // 2:hi // 2] = ret_s[slot, lo // 2:hi // 2]

    tab[0].wait()
    for f in VEC:
        wait_chunk(f)
        merge(*bounds("D", f))
        field_x(f, f)
    for f in VEC:
        curl_x(f)
    tab[1].wait()
    lax.fori_loop(0, 6, lambda f, carry: (to_grid(f), carry)[1], 0)
    tab[2].wait()
    tab[3].wait()
    for c in VEC:
        cross(c)
        from_x(c)
    project()
    for chunk in PAIR:
        unmerge(RET_CHUNKS[chunk], RET_CHUNKS[chunk + 1])
        send_back(chunk)
    wait_chunk(3)
    merge(*bounds("D", 3))
    field_x(6, 3)
    to_grid(6)
    for c in VEC:
        flux(c)
        from_x(c)
    diverge()
    unmerge(*RET_CHUNKS[2:])
    send_back(2)

    for kind, mine in (("D", dense), ("S", sparse)):
        @pl.when(mine)
        def _():
            for k in PEERS:
                pr, pc = peer(k)
                for chunk in FIELDS:
                    out_copy(kind, chunk, my_slot, pr, pc, me).wait_send()
                for chunk in VEC:
                    ret_copy(kind, chunk, 0, pr, pc, dev_of(pr, pc)).wait_recv()

    for kind, slot, r, c in everyone():
        @pl.when(me != dev_of(r, c))
        def _():
            for chunk in VEC:
                ret_copy(kind, chunk, slot, r, c, me).wait_send()


def out_kernel(back, tab_hbm, ore, oim, tre, tim, buf, tab, sem, tab_sem):
    row, col = lax.axis_index("row"), lax.axis_index("col")
    dense = jnp.logical_or(row == 0, row == 3)
    load = pltpu.make_async_copy(tab_hbm.at[dev_of(row, col)], tab, tab_sem)
    load.start()
    odd = lax.broadcasted_iota(jnp.int32, (1, LANES), 1) % FLOWS >= N
    for f in FIELDS:
        for ri in PAIR:
            buf[f, ri, LOW_ROWS:2 * LOW_ROWS, :] = jnp.zeros((LOW_ROWS, FLOWS), F32)

    @pl.when(jnp.logical_not(dense))
    def _():
        for f in FIELDS:
            for ri in PAIR:
                for a, size in ((0, LOW_ROWS), (2 * LOW_ROWS, ROWS - 2 * LOW_ROWS)):
                    buf[f, ri, pl.ds(a, size), :] = jnp.zeros((size, FLOWS), F32)
    load.wait()

    def place(ri, b, kind, f, i, tile, block):
        first = SLOTS[i] * FLOWS + b
        if kind == "D":
            buf[f, ri, pl.ds(first, N, stride=2), :] = tile[N * block:N * block + N]
        else:
            at = N // 2 * (2 * (block % QUAD) + block // QUAD)
            first = first + jnp.where(row == 1, 0, N)
            buf[f, ri, pl.ds(first, HALF, stride=2), :] = tile[at:at + HALF]

    def rebuild(ri, kind):
        per = QUAD if kind == "D" else OCT
        tiles = D_RET if kind == "D" else S_RET
        mixed = -(-2 * KEPT // per)

        def body(b, carry):
            held = None
            for t in range(tiles):
                v = back[:, t, 2 * ri + b].reshape(FLOWS, LANES)
                if t < mixed:
                    k = [tab[pl.ds((b * S_OUT + t) * 3 + q, 1)] for q in VEC]
                    other = jnp.where(odd, roll(v, N), roll(v, -N))
                    out = (v * k[0] + other * k[1]).T
                    z = v * k[2]
                    if t % 2 == 0:
                        held = z
                    if t % 2 == 1 or t == mixed - 1:
                        last = t % 2 == 1
                        zt = (jnp.where(odd, held, roll(z, -N)) if last else z).T
                        for back_by, shift in ((1, 0), (0, 1)) if last else ((0, 0),):
                            for s in range(1, per, 2):
                                n = per * (t - back_by) + s
                                if n < 2 * KEPT:
                                    place(ri, b, kind, 2, n // 2, zt, s - shift)
                else:
                    out = v.T
                for s in range(per):
                    n = per * t + s
                    if n < 2 * KEPT:
                        place(ri, b, kind, n % 2, n // 2, out, s)
                    elif n < 3 * KEPT:
                        place(ri, b, kind, 3, n - 2 * KEPT, out, s)
            return carry
        lax.fori_loop(0, 2, body, 0)

    copies = []
    for ri in PAIR:
        @pl.when(dense)
        def _():
            rebuild(ri, "D")

        @pl.when(jnp.logical_not(dense))
        def _():
            rebuild(ri, "S")

        for f in FIELDS:
            dst = (ore, oim)[ri].at[f] if f < 3 else (tre, tim)[ri].at[0]
            copies.append(pltpu.make_async_copy(buf.at[f, ri], dst, sem.at[f, ri]))
            copies[-1].start()
    for cp in copies:
        cp.wait()


def solution(mesh):
    spec_vec = P('ens', None, None, 'row', 'col')
    spec_scal = P('ens', None, 'row', 'col')
    consts = tables()
    src_np = source_tables()
    vmem = pl.BlockSpec(memory_space=pltpu.VMEM)
    hbm = pl.BlockSpec(memory_space=pl.ANY)
    dma = pltpu.SemaphoreType.DMA
    links = dma((OCT, QUAD))

    def f32(*lead):
        return pltpu.VMEM((*lead, *TILE), F32)

    def local_term(vel_re, vel_im, scal_re, scal_im):
        vec = [jnp.transpose(a, (1, 2, 3, QUAD, 0)).reshape(3, ROWS, FLOWS) for a in (vel_re, vel_im)]
        scal = [jnp.transpose(a, (1, 2, 3, 0)).reshape(1, ROWS, FLOWS) for a in (scal_re, scal_im)]
        back = pl.pallas_call(
            main_kernel,
            out_shape=jax.ShapeDtypeStruct((OCT, D_RET, QUAD, *TILE), F32),
            in_specs=[hbm] * OCT,
            out_specs=vmem,
            scratch_shapes=[
                pltpu.VMEM((2, QUAD * KEPT_ROWS + QUAD * FLOWS, FLOWS), F32), f32(OCT, D_OUT, QUAD), f32(QUAD, D_OUT, QUAD), f32(QUAD, S_OUT, QUAD),
                f32(QUAD, QUAD * KEPT), pltpu.VMEM((7, 2, 2, K, 3 * LANES), BF16), pltpu.VMEM((7, QUAD, K, K), F32),
                pltpu.VMEM((2, 2, 3, K, K), BF16), pltpu.VMEM((3, 2, 2, K, LANES), F32), f32(3, QUAD, KEPT),
                f32(QUAD, QUAD * D_RET), f32(QUAD, D_RET, QUAD), f32(QUAD, S_RET, QUAD),
                *[pltpu.VMEM(a.shape, a.dtype) for a in consts],
                dma((QUAD, 2, 2)), dma((QUAD,)), links, links, links, links,
            ],
            compiler_params=pltpu.CompilerParams(
                collective_id=0, has_side_effects=True, vmem_limit_bytes=60 * MIB),
            name="flow_home",
        )(*vec, *scal, *[jnp.asarray(a) for a in consts])
        outs = pl.pallas_call(
            out_kernel,
            out_shape=[jax.ShapeDtypeStruct((c, ROWS, FLOWS), F32) for c in (3, 3, 1, 1)],
            in_specs=[vmem, hbm],
            out_specs=[hbm] * QUAD,
            scratch_shapes=[pltpu.VMEM((QUAD, 2, ROWS, FLOWS), F32), pltpu.VMEM(src_np.shape[1:], F32), dma((QUAD, 2)), dma],
            compiler_params=pltpu.CompilerParams(vmem_limit_bytes=40 * MIB),
            name="lay_out",
        )(back, jnp.asarray(src_np))
        out_v = [jnp.transpose(a.reshape(3, N, OCT, OCT, FLOWS), (QUAD, 0, 1, 2, 3)) for a in outs[:2]]
        out_s = [jnp.transpose(a.reshape(N, OCT, OCT, FLOWS), (3, 0, 1, 2)) for a in outs[2:]]
        return (*out_v, *out_s)

    return jax.shard_map(local_term, mesh=mesh, in_specs=(spec_vec, spec_vec, spec_scal, spec_scal),
                         out_specs=(spec_vec, spec_vec, spec_scal, spec_scal), check_vma=False)
```

time: 1080 us -> 63.7 us (0.06)
  local copies, waits for them, and re-layouts: 316 us -> 1.59 us
  matrix products: 231 us -> 0 us
  other arithmetic: 205 us -> 0 us
  blocking collectives: 166 us -> 0 us
  waiting for transfers between devices: 142 us -> 0 us
  Pallas kernels: 0 us -> 61.3 us
  starting transfers between devices: 14.4 us -> 0 us
    another operation x18 -> x0, matrix products: 231 us -> none  [the longest x3 68.8 us: local_term(): physical = jnp.fft.irfft(spectra, n=grid_n, axis=4, norm='ortho')]
    all_to_all x2 -> x0, blocking collectives: 166 us -> none  [exchange(): lax.all_to_all(wire_pair, axis_name, split_axis + 1, concat_axis + 1, til...]
    all_to_all x2 -> x0, waiting for transfers between devices: 142 us -> none  [exchange(): lax.all_to_all(wire_pair, axis_name, split_axis + 1, concat_axis + 1, til...]
    unnamed x59 -> x4, local copies, waits for them, and re-layouts: 141 us -> 1.59 us
    another operation x10 -> x0, local copies, waits for them, and re-layouts: 104 us -> none  [the longest x4 67.2 us: exchange(): wire_pair = jnp.stack([jnp.real(spectra), jnp.imag(spectra)])]
    all_to_all x4 -> x0, other arithmetic: 95 us -> none  [exchange(): lax.all_to_all(wire_pair, axis_name, split_axis + 1, concat_axis + 1, til...]
    another operation x10 -> x0, other arithmetic: 74.6 us -> none  [the longest x5 52 us: exchange(): wire_pair = jnp.stack([jnp.real(spectra), jnp.imag(spectra)])]
    pallas_call x0 -> x2, Pallas kernels: none -> 61.3 us  [the longest x1 56.6 us: local_term(): pl.pallas_call(main_kernel, out_shape=jax.ShapeDtypeStruct((OCT, D_RET, Q...]
  transfers between devices with their start and end apart: 2 -> 0, of which waited for: 2 -> 0; matrix products, arithmetic and copies ran while one was open for 1% -> 0% of each run, Pallas kernels for 0% -> 0%
where the time goes in v2:
time: 63.7 us; the launch traced here: 63.6 us
  Pallas kernels  61.3 us (96%)
  local copies, waits for them, and re-layouts  1.59 us (2%)
  between operations  0.66 us (1%)
    pallas_call x1, Pallas kernels, local_term(): pl.pallas_call(main_kernel, out_shape=jax.ShapeDtypeStruct((OCT, D_RET, Q...  56.6 us
    pallas_call x1, Pallas kernels, local_term(): pl.pallas_call(out_kernel, out_shape=[jax.ShapeDtypeStruct((c, ROWS, FLOW...  4.73 us
    unnamed x4, local copies, waits for them, and re-layouts  1.59 us

profile of v2, /device:TPU:1, one launch (start us, length us, event | category | flops | bytes accessed | tf_op | source)
XLA Modules:
  0.0 63.6 jit_solution(8035928489586731085)
XLA Ops:
  0.6 0.0 copy-start.1
  0.6 56.6 %flow_home.1.back = f32[8,16,4,8,128]{4,3,2,1,0:T(8,128)} custom-call(f32[3,2048,64]{2,1,0:T(8,128)} %bitcast.24, f32[3,2048,64]{2,1,0:T(8,128)} %bitcast.25, f32[1,2048,64]{2,1,0:T(8,128)} %bitcast.26, f32[1,2048,64]{2,1,0:T(8,128)} %bitcast.27, bf16[2,2,3,256,256]{4,3,2,1,0:T(8,128)(2,1)} %constant.10.clone.inv_hbm, ...), custom_call_target="tpu_custom_call" | custom-call | tf_op jit(solution)/shard_map/flow_home/pallas_call | solution.py:629
  57.3 0.0 copy-done.1
  57.3 0.0 copy-start
  57.3 1.6 %copy-done = f32[8,16,4,8,128]{4,3,2,1,0:T(8,128)S(1)} copy-done((f32[8,16,4,8,128]{4,3,2,1,0:T(8,128)S(1)}, f32[8,16,4,8,128]{4,3,2,1,0:T(8,128)}, u32[]{:S(2)}) %copy-start) | copy-done | bytes 2097176
  58.9 4.7 %lay_out.1 = (f32[3,2048,64]{2,1,0:T(8,128)}, f32[3,2048,64]{2,1,0:T(8,128)}, f32[1,2048,64]{2,1,0:T(8,128)}, f32[1,2048,64]{2,1,0:T(8,128)}) custom-call(f32[8,16,4,8,128]{4,3,2,1,0:T(8,128)S(1)} %copy-done, f32[8,66,128]{2,1,0:T(8,128)S(1)} %copy-done.1), custom_call_target="tpu_custom_call" | custom-call | tf_op jit(solution)/shard_map/lay_out/pallas_call | solution.py:646
Async XLA Ops:
  0.6 56.6 %copy-start.1 = (f32[8,66,128]{2,1,0:T(8,128)S(1)}, f32[8,66,128]{2,1,0:T(8,128)}, u32[]{:S(2)}) copy-start(f32[8,66,128]{2,1,0:T(8,128)} %constant.14.clone.tab_hbm) | copy-start | bytes 811012
  57.3 1.6 %copy-start = (f32[8,16,4,8,128]{4,3,2,1,0:T(8,128)S(1)}, f32[8,16,4,8,128]{4,3,2,1,0:T(8,128)}, u32[]{:S(2)}) copy-start(f32[8,16,4,8,128]{4,3,2,1,0:T(8,128)} %flow_home.1.back) | copy-start | bytes 6291460

commit v3 on v2

--- a/solution.py
+++ b/solution.py
@@ -114,8 +114,7 @@
         got = home_mode(lane, 0)
         if got is not None and got[1] == 0:
             weight[0, 0, lane] = 1.0
-    hi, mid, low = split3(inv * weight)
-    inv3 = np.stack([np.concatenate(pair, axis=2) for pair in ((hi, low), (mid, mid), (hi, hi))], axis=2)
+    inv3 = np.stack(split3(inv * weight))
     fwd3 = np.concatenate(split3(fwd), axis=3)
     return inv3, fwd3, wave, home.reshape(-1, LANES)
 
@@ -198,7 +197,7 @@
 
 def main_kernel(vre, vim, sre, sim, inv_hbm, fwd_hbm, wave_hbm, home_hbm, back,
                 xin, send, recv_d, recv_s, merged, lhs, phys, prod, spec, bins, res, ret_d, ret_s,
-                inv, fwd, wave, home, in_sem, tab_sem, s1, r1, s2, r2):
+                inv, fwd, wave, home, in_sem, tab_sem, own_sem, s1, r1, s2, r2):
     row, col, ens = lax.axis_index("row"), lax.axis_index("col"), lax.axis_index("ens")
     me = dev_of(row, col)
     dense = jnp.logical_or(row == 0, row == 3)
@@ -214,8 +213,10 @@
                     src.at[pl.ds(a, size)], xin.at[ri, pl.ds(KEPT_ROWS * f + b, size)], in_sem.at[f, ri, half])
                 cp.start()
                 loads.append(cp)
-    tab = [pltpu.make_async_copy(src, dst, tab_sem.at[i]) for i, (src, dst) in enumerate(
-        ((wave_hbm, wave), (inv_hbm, inv), (fwd_hbm, fwd), (home_hbm, home)))]
+    wanted = [(wave_hbm, wave), (fwd_hbm, fwd), (home_hbm, home)]
+    wanted += [(inv_hbm.at[part], inv.at[:, :, pair, pl.ds(LANES * h, LANES)])
+               for pair, parts in enumerate(((0, 2), (1, 1), (0, 0))) for h, part in enumerate(parts)]
+    tab = [pltpu.make_async_copy(src, dst, tab_sem.at[i]) for i, (src, dst) in enumerate(wanted)]
     for cp in tab:
         cp.start()
 
@@ -375,7 +376,7 @@
     def to_spec(c):
         for b in PAIR:
             for ri in PAIR:
-                hi, mid, lo = (prod[b, ri, p] for p in VEC)
+                hi, mid, lo = (prod[c, b, ri, p] for p in VEC)
                 both = dot(hi, fwd[b, ri, :, 0:K]) + dot(mid, fwd[b, ri, :, 0:K])
                 small = dot(lo, fwd[b, ri, :, 0:LANES]) + dot(hi, fwd[b, ri, :, K:])
                 spec[c, b, ri] = small + both[:, LANES:] + both[:, :LANES]
@@ -389,10 +390,9 @@
                 for ri in PAIR:
                     v = side[0] - side[1] if ri else side[0] + side[1]
                     for p, part in enumerate(split_bf16(v)):
-                        prod[b, ri, p, rows, :] = part
+                        prod[c, b, ri, p, rows, :] = part
             return carry
         lax.fori_loop(0, HALF, body, 0, unroll=2)
-        to_spec(c)
 
     def cross(c):
         c1, c2 = (c + 1) % 3, (c + 2) % 3
@@ -460,13 +460,19 @@
             return carry
         lax.fori_loop(0, QUAD, body, 0)
 
-    def ret_copy(kind, chunk, slot, r, c, frm):
+    def ret_part(kind, chunk):
         lo, hi = RET_CHUNKS[chunk], RET_CHUNKS[chunk + 1]
         if kind == "S":
             lo, hi = lo // 2, hi // 2
-        part = pl.ds(lo, hi - lo)
-        src = ret_d if kind == "D" else ret_s
+        return ret_d if kind == "D" else ret_s, pl.ds(lo, hi - lo)
+
+    def ret_copy(kind, chunk, slot, r, c, frm):
+        src, part = ret_part(kind, chunk)
         return remote(src.at[slot, part], back.at[frm, part], (s2, r2), dev_of(r, c), frm, chunk, r, c)
+
+    def own_copy(kind, chunk, slot, d):
+        src, part = ret_part(kind, chunk)
+        return pltpu.make_async_copy(src.at[slot, part], back.at[d, part], own_sem.at[chunk])
 
     def send_back(chunk):
         for kind, slot, r, c in everyone():
@@ -478,25 +484,31 @@
 
             @pl.when(me == d)
             def _():
-                lo, hi = RET_CHUNKS[chunk], RET_CHUNKS[chunk + 1]
-                if kind == "D":
-                    back[d, lo:hi] = ret_d[slot, lo:hi]
-                else:
-                    back[d, lo // 2:hi // 2] = ret_s[slot, lo // 2:hi // 2]
+                own_copy(kind, chunk, slot, d).start()
 
     tab[0].wait()
     for f in VEC:
         wait_chunk(f)
         merge(*bounds("D", f))
         field_x(f, f)
+        if f == 0:
+            for cp in tab[3:]:
+                cp.wait()
+            to_grid(0)
+        elif f == 1:
+            curl_x(2)
+            to_grid(1)
+            to_grid(5)
+    curl_x(0)
+    curl_x(1)
     for f in VEC:
-        curl_x(f)
+        to_grid(2 + f)
     tab[1].wait()
-    lax.fori_loop(0, 6, lambda f, carry: (to_grid(f), carry)[1], 0)
     tab[2].wait()
-    tab[3].wait()
     for c in VEC:
         cross(c)
+    for c in VEC:
+        to_spec(c)
         from_x(c)
     project()
     for chunk in PAIR:
@@ -508,6 +520,8 @@
     to_grid(6)
     for c in VEC:
         flux(c)
+    for c in VEC:
+        to_spec(c)
         from_x(c)
     diverge()
     unmerge(*RET_CHUNKS[2:])
@@ -524,28 +538,47 @@
                     ret_copy(kind, chunk, 0, pr, pc, dev_of(pr, pc)).wait_recv()
 
     for kind, slot, r, c in everyone():
-        @pl.when(me != dev_of(r, c))
+        d = dev_of(r, c)
+
+        @pl.when(me != d)
         def _():
             for chunk in VEC:
                 ret_copy(kind, chunk, slot, r, c, me).wait_send()
 
-
-def out_kernel(back, tab_hbm, ore, oim, tre, tim, buf, tab, sem, tab_sem):
+        @pl.when(me == d)
+        def _():
+            for chunk in VEC:
+                own_copy(kind, chunk, slot, d).wait()
+
+
+def out_kernel(back_hbm, tab_hbm, ore, oim, tre, tim, buf, tab, back, blank, sem, in_sem, tab_sem):
     row, col = lax.axis_index("row"), lax.axis_index("col")
     dense = jnp.logical_or(row == 0, row == 3)
+    loads = [pltpu.make_async_copy(back_hbm.at[:, :, pl.ds(2 * ri, 2)], back.at[:, :, pl.ds(2 * ri, 2)], in_sem.at[ri])
+             for ri in PAIR]
     load = pltpu.make_async_copy(tab_hbm.at[dev_of(row, col)], tab, tab_sem)
-    load.start()
+    for cp in (*loads, load):
+        cp.start()
     odd = lax.broadcasted_iota(jnp.int32, (1, LANES), 1) % FLOWS >= N
+
+    def store(f, ri, which):
+        first = (0, LOW_ROWS, 2 * LOW_ROWS)[which]
+        part = pl.ds(first, LOW_ROWS if which < 2 else ROWS - first)
+        dst = (ore, oim)[ri].at[f] if f < 3 else (tre, tim)[ri].at[0]
+        src = blank if which == 1 else buf.at[f, ri, part]
+        return pltpu.make_async_copy(src, dst.at[part], sem.at[f, ri, which])
+
+    blank[...] = jnp.zeros_like(blank)
     for f in FIELDS:
         for ri in PAIR:
-            buf[f, ri, LOW_ROWS:2 * LOW_ROWS, :] = jnp.zeros((LOW_ROWS, FLOWS), F32)
+            store(f, ri, 1).start()
 
     @pl.when(jnp.logical_not(dense))
     def _():
         for f in FIELDS:
             for ri in PAIR:
-                for a, size in ((0, LOW_ROWS), (2 * LOW_ROWS, ROWS - 2 * LOW_ROWS)):
-                    buf[f, ri, pl.ds(a, size), :] = jnp.zeros((size, FLOWS), F32)
+                for first, size in ((0, LOW_ROWS), (2 * LOW_ROWS, ROWS - 2 * LOW_ROWS)):
+                    buf[f, ri, pl.ds(first, size), :] = jnp.zeros((size, FLOWS), F32)
     load.wait()
 
     def place(ri, b, kind, f, i, tile, block):
@@ -562,25 +595,25 @@
         tiles = D_RET if kind == "D" else S_RET
         mixed = -(-2 * KEPT // per)
 
-        def body(b, carry):
-            held = None
-            for t in range(tiles):
+        held = [None, None]
+        ends = (5, 10, 13, 15) if kind == "D" else (3, 5, 6, 7)
+        for t in range(tiles):
+            for b in PAIR:
                 v = back[:, t, 2 * ri + b].reshape(FLOWS, LANES)
                 if t < mixed:
                     k = [tab[pl.ds((b * S_OUT + t) * 3 + q, 1)] for q in VEC]
                     other = jnp.where(odd, roll(v, N), roll(v, -N))
                     out = (v * k[0] + other * k[1]).T
                     z = v * k[2]
-                    if t % 2 == 0:
-                        held = z
-                    if t % 2 == 1 or t == mixed - 1:
-                        last = t % 2 == 1
-                        zt = (jnp.where(odd, held, roll(z, -N)) if last else z).T
+                    last = t % 2 == 1
+                    if last or t == mixed - 1:
+                        zt = (jnp.where(odd, held[b], roll(z, -N)) if last else z).T
                         for back_by, shift in ((1, 0), (0, 1)) if last else ((0, 0),):
                             for s in range(1, per, 2):
                                 n = per * (t - back_by) + s
                                 if n < 2 * KEPT:
                                     place(ri, b, kind, 2, n // 2, zt, s - shift)
+                    held[b] = z
                 else:
                     out = v.T
                 for s in range(per):
@@ -589,11 +622,14 @@
                         place(ri, b, kind, n % 2, n // 2, out, s)
                     elif n < 3 * KEPT:
                         place(ri, b, kind, 3, n - 2 * KEPT, out, s)
-            return carry
-        lax.fori_loop(0, 2, body, 0)
-
-    copies = []
+            if t in ends:
+                e = ends.index(t)
+                for f in VEC if e < 2 else (3,):
+                    store(f, ri, 2 * (e % 2)).start()
+
     for ri in PAIR:
+        loads[ri].wait()
+
         @pl.when(dense)
         def _():
             rebuild(ri, "D")
@@ -601,13 +637,10 @@
         @pl.when(jnp.logical_not(dense))
         def _():
             rebuild(ri, "S")
-
-        for f in FIELDS:
-            dst = (ore, oim)[ri].at[f] if f < 3 else (tre, tim)[ri].at[0]
-            copies.append(pltpu.make_async_copy(buf.at[f, ri], dst, sem.at[f, ri]))
-            copies[-1].start()
-    for cp in copies:
-        cp.wait()
+    for f in FIELDS:
+        for ri in PAIR:
+            for which in VEC:
+                store(f, ri, which).wait()
 
 
 def solution(mesh):
@@ -615,7 +648,6 @@
     spec_scal = P('ens', None, 'row', 'col')
     consts = tables()
     src_np = source_tables()
-    vmem = pl.BlockSpec(memory_space=pltpu.VMEM)
     hbm = pl.BlockSpec(memory_space=pl.ANY)
     dma = pltpu.SemaphoreType.DMA
     links = dma((OCT, QUAD))
@@ -630,14 +662,14 @@
             main_kernel,
             out_shape=jax.ShapeDtypeStruct((OCT, D_RET, QUAD, *TILE), F32),
             in_specs=[hbm] * OCT,
-            out_specs=vmem,
+            out_specs=hbm,
             scratch_shapes=[
                 pltpu.VMEM((2, QUAD * KEPT_ROWS + QUAD * FLOWS, FLOWS), F32), f32(OCT, D_OUT, QUAD), f32(QUAD, D_OUT, QUAD), f32(QUAD, S_OUT, QUAD),
                 f32(QUAD, QUAD * KEPT), pltpu.VMEM((7, 2, 2, K, 3 * LANES), BF16), pltpu.VMEM((7, QUAD, K, K), F32),
-                pltpu.VMEM((2, 2, 3, K, K), BF16), pltpu.VMEM((3, 2, 2, K, LANES), F32), f32(3, QUAD, KEPT),
+                pltpu.VMEM((3, 2, 2, 3, K, K), BF16), pltpu.VMEM((3, 2, 2, K, LANES), F32), f32(3, QUAD, KEPT),
                 f32(QUAD, QUAD * D_RET), f32(QUAD, D_RET, QUAD), f32(QUAD, S_RET, QUAD),
-                *[pltpu.VMEM(a.shape, a.dtype) for a in consts],
-                dma((QUAD, 2, 2)), dma((QUAD,)), links, links, links, links,
+                pltpu.VMEM((2, 2, 3, K, K), BF16), *[pltpu.VMEM(a.shape, a.dtype) for a in consts[1:]],
+                dma((QUAD, 2, 2)), dma((9,)), dma((3,)), links, links, links, links,
             ],
             compiler_params=pltpu.CompilerParams(
                 collective_id=0, has_side_effects=True, vmem_limit_bytes=60 * MIB),
@@ -646,10 +678,11 @@
         outs = pl.pallas_call(
             out_kernel,
             out_shape=[jax.ShapeDtypeStruct((c, ROWS, FLOWS), F32) for c in (3, 3, 1, 1)],
-            in_specs=[vmem, hbm],
+            in_specs=[hbm, hbm],
             out_specs=[hbm] * QUAD,
-            scratch_shapes=[pltpu.VMEM((QUAD, 2, ROWS, FLOWS), F32), pltpu.VMEM(src_np.shape[1:], F32), dma((QUAD, 2)), dma],
-            compiler_params=pltpu.CompilerParams(vmem_limit_bytes=40 * MIB),
+            scratch_shapes=[pltpu.VMEM((QUAD, 2, ROWS, FLOWS), F32), pltpu.VMEM(src_np.shape[1:], F32),
+                            f32(OCT, D_RET, QUAD), pltpu.VMEM((LOW_ROWS, FLOWS), F32), dma((QUAD, 2, 3)), dma((2,)), dma],
+            compiler_params=pltpu.CompilerParams(vmem_limit_bytes=60 * MIB),
             name="lay_out",
         )(back, jnp.asarray(src_np))
         out_v = [jnp.transpose(a.reshape(3, N, OCT, OCT, FLOWS), (QUAD, 0, 1, 2, 3)) for a in outs[:2]]

time: 63.7 us -> 59.7 us (0.937)
  Pallas kernels: 61.3 us -> 58.6 us
  local copies, waits for them, and re-layouts: 1.59 us -> 0 us
    pallas_call x1, Pallas kernels: 56.6 us -> 53 us  [local_term(): pl.pallas_call(main_kernel, out_shape=jax.ShapeDtypeStruct((OCT, D_RET, Q...]
    unnamed x4 -> x0, local copies, waits for them, and re-layouts: 1.59 us -> none
    pallas_call x1, Pallas kernels: 4.73 us -> 5.64 us  [local_term(): pl.pallas_call(out_kernel, out_shape=[jax.ShapeDtypeStruct((c, ROWS, FLOW...]
where the time goes in v3:
time: 59.7 us; the launch traced here: 59.4 us
  Pallas kernels  58.6 us (98%)
  between operations  0.8 us (1%)
    pallas_call x1, Pallas kernels, local_term(): pl.pallas_call(main_kernel, out_shape=jax.ShapeDtypeStruct((OCT, D_RET, Q...  53 us
    pallas_call x1, Pallas kernels, local_term(): pl.pallas_call(out_kernel, out_shape=[jax.ShapeDtypeStruct((c, ROWS, FLOW...  5.64 us

profile of v3, /device:TPU:1, one launch (start us, length us, event | category | flops | bytes accessed | tf_op | source)
XLA Modules:
  0.0 59.4 jit_solution(14096334395979085576)
XLA Ops:
  0.6 53.0 %flow_home.1.back_hbm = f32[8,16,4,8,128]{4,3,2,1,0:T(8,128)} custom-call(f32[3,2048,64]{2,1,0:T(8,128)} %bitcast.24, f32[3,2048,64]{2,1,0:T(8,128)} %bitcast.25, f32[1,2048,64]{2,1,0:T(8,128)} %bitcast.26, f32[1,2048,64]{2,1,0:T(8,128)} %bitcast.27, bf16[3,2,2,128,256]{4,3,2,1,0:T(8,128)(2,1)} %constant.10.clone.inv_hbm, ...), custom_call_target="tpu_custom_call" | custom-call | tf_op jit(solution)/shard_map/flow_home/pallas_call | solution.py:661
  53.6 5.6 %lay_out.1 = (f32[3,2048,64]{2,1,0:T(8,128)}, f32[3,2048,64]{2,1,0:T(8,128)}, f32[1,2048,64]{2,1,0:T(8,128)}, f32[1,2048,64]{2,1,0:T(8,128)}) custom-call(f32[8,16,4,8,128]{4,3,2,1,0:T(8,128)} %flow_home.1.back_hbm, f32[8,66,128]{2,1,0:T(8,128)} %constant.14.clone.tab_hbm), custom_call_target="tpu_custom_call" | custom-call | tf_op jit(solution)/shard_map/lay_out/pallas_call | solution.py:678

commit v4 on v3

--- a/solution.py
+++ b/solution.py
@@ -17,6 +17,7 @@
 TINY = 1e-9
 MIB = 1 << 20
 QUAD, OCT, HALF = 4, 8, 16
+PARTS = RE, IM = slice(0, 2), slice(2, 4)
 PAIR, VEC, FIELDS, PEERS = range(2), range(3), range(QUAD), range(1, OCT)
 MESH = pl.DeviceIdType.MESH
 F32 = jnp.float32
@@ -29,8 +30,7 @@
 D_OUT, S_OUT, D_RET, S_RET = 21, 11, HALF, OCT
 D_CHUNKS, S_CHUNKS = (0, 6, 11, HALF, 21), (0, 3, 6, OCT, 11)
 RET_CHUNKS = (0, QUAD, 10, HALF)
-DENSE = [(0, 0), (3, 0), (0, 1), (3, 1)]
-SPARSE = [(1, 0), (2, 0), (1, 1), (2, 1)]
+DENSE, SPARSE = ([(r, c) for c in PAIR for r in rows] for rows in ((0, 3), (1, 2)))
 
 
 def mode(j):
@@ -94,7 +94,7 @@
     yy, zz = np.array(points).T
     inv = np.zeros((2, 2, LANES, K))
     wave = np.zeros((2, QUAD, LANES), np.float32)
-    home = np.zeros((2, KEPT, 5, LANES), np.float32)
+    home = np.zeros((2, 5, KEPT, 1, LANES), np.float32)
     for parity in PAIR:
         for lane in range(LANES):
             got = home_mode(lane, parity)
@@ -107,7 +107,7 @@
             wave[parity, :, lane] = ky * UNIT, kz * UNIT, math.cos(UNIT * ky / 2), math.sin(UNIT * ky / 2)
             for i, j in enumerate(SLOTS):
                 e1, e2 = basis(mode(j), ky, kz)
-                home[parity, i, :, lane] = *e1[:2], *e2
+                home[parity, :, i, 0, lane] = *e1[:2], *e2
     fwd = np.swapaxes(inv, 2, 3)
     weight = np.full((2, 1, LANES, 1), 2.0)
     for lane in range(LANES):
@@ -116,7 +116,7 @@
             weight[0, 0, lane] = 1.0
     inv3 = np.stack(split3(inv * weight))
     fwd3 = np.concatenate(split3(fwd), axis=3)
-    return inv3, fwd3, wave, home.reshape(-1, LANES)
+    return inv3, fwd3, wave, home
 
 
 def source_tables():
@@ -191,8 +191,14 @@
     return col * QUAD + row
 
 
+def unrolled(n):
+    def run(body):
+        lax.fori_loop(0, n, lambda i, carry: (body(i), carry)[1], 0, unroll=True)
+    return run
+
+
 def roll(x, shift):
-    return pltpu.roll(x, shift % LANES, 1)
+    return pltpu.roll(x, shift % LANES, x.ndim - 1)
 
 
 def main_kernel(vre, vim, sre, sim, inv_hbm, fwd_hbm, wave_hbm, home_hbm, back,
@@ -234,8 +240,8 @@
 
     def pack_dense(lo, hi):
         def body(n, carry):
-            t, rb = n // QUAD, n % QUAD
-            blk = xin[rb // 2, pl.ds(t * K + rb % 2, LANES, stride=2), :]
+            t, rb = lax.div(n, QUAD), lax.rem(n, QUAD)
+            blk = xin[lax.div(rb, 2), pl.ds(t * K + lax.rem(rb, 2), LANES, stride=2), :]
             send[:, t, rb] = blk.T.reshape(OCT, *TILE)
             return carry
         lax.fori_loop(QUAD * lo, QUAD * hi, body, 0, unroll=QUAD)
@@ -244,9 +250,9 @@
         first = jnp.where(row == 1, 0, N)
 
         def body(n, carry):
-            t, rb = n // QUAD, n % QUAD
-            base = t * OCT * FLOWS + first + rb % 2
-            parts = [xin[rb // 2, pl.ds(base + (p // 2 + QUAD * (p % 2)) * FLOWS, HALF, stride=2), :] for p in range(OCT)]
+            t, rb = lax.div(n, QUAD), lax.rem(n, QUAD)
+            base, ri = t * OCT * FLOWS + first + lax.rem(rb, 2), lax.div(rb, 2)
+            parts = [xin[ri, pl.ds(base + (p // 2 + QUAD * (p % 2)) * FLOWS, HALF, stride=2), :] for p in range(OCT)]
             send[:, t, rb] = jnp.concatenate(parts, axis=0).T.reshape(OCT, *TILE)
             return carry
         lax.fori_loop(QUAD * lo, QUAD * hi, body, 0, unroll=QUAD)
@@ -298,8 +304,8 @@
 
     def swap_blocks(tiles, forward):
         def outer(a, b, c, d):
-            return (jnp.where(left, a, roll(c, FLOWS)), jnp.where(left, b, roll(d, FLOWS)),
-                    jnp.where(left, roll(a, FLOWS), c), jnp.where(left, roll(b, FLOWS), d))
+            ca, db = roll(jnp.where(left, c, a), FLOWS), roll(jnp.where(left, d, b), FLOWS)
+            return jnp.where(left, a, ca), jnp.where(left, b, db), jnp.where(left, ca, c), jnp.where(left, db, d)
 
         def inner(a, b, c, d):
             return (jnp.where(even, a, roll(b, N)), jnp.where(even, roll(a, -N), b),
@@ -307,158 +313,136 @@
         return inner(*outer(*tiles)) if forward else outer(*inner(*tiles))
 
     def merge(lo, hi):
-        def body(b, carry):
-            cos, sin = wave[b, pl.ds(2, 1)], wave[b, pl.ds(3, 1)]
-            for t in range(lo, hi):
-                got = []
-                for ri in PAIR:
-                    rb = 2 * ri + b
-                    d = [recv_d[o, t, rb] for o in FIELDS]
-                    s = [recv_s[o, t // 2, rb] for o in FIELDS]
-                    h = HALF * (t % 2)
-                    c1 = jnp.where(low, d[2], roll(d[3], 2))
-                    s0 = roll(s[0], -h) if h else s[0]
-                    rest = jnp.where(low, roll(s[2], 20 - h), roll(s[3], 14 - h))
-                    s1_ = jnp.where(p32 < 12, s0, jnp.where(p32 < 20, roll(s[1], QUAD - h), rest))
-                    got.append(swap_blocks((d[0], d[1], c1, s1_), True))
-                for s, (re, im) in enumerate(zip(*got)):
-                    merged[b, QUAD * t + s] = re * cos + im * sin
-                    merged[2 + b, QUAD * t + s] = im * cos - re * sin
-            return carry
-        lax.fori_loop(0, 2, body, 0)
-
-    def to_x(f, b, get):
+        cos, sin = wave[:, pl.ds(2, 1)], wave[:, pl.ds(3, 1)]
+        for t in range(lo, hi):
+            got = []
+            for part in PARTS:
+                d = [recv_d[o, t, part] for o in FIELDS]
+                s = [recv_s[o, t // 2, part] for o in FIELDS]
+                h = HALF * (t % 2)
+                c1 = jnp.where(low, d[2], roll(d[3], 2))
+                s0 = roll(s[0], -h) if h else s[0]
+                rest = jnp.where(low, roll(s[2], 20 - h), roll(s[3], 14 - h))
+                s1_ = jnp.where(p32 < 12, s0, jnp.where(p32 < 20, roll(s[1], QUAD - h), rest))
+                got.append(swap_blocks((d[0], d[1], c1, s1_), True))
+            for s, (re, im) in enumerate(zip(*got)):
+                merged[RE, QUAD * t + s] = re * cos + im * sin
+                merged[IM, QUAD * t + s] = im * cos - re * sin
+
+    def to_x(f, get):
         vals = [None] * N
         for i, j in enumerate(SLOTS):
             vals[j] = get(i)
         out = fft(vals, 1)
         for x in range(0, N, 2):
             for ri in PAIR:
-                hi, mid, lo = split_bf16(jnp.concatenate([out[x][ri], out[x + 1][ri]], axis=0))
+                hi, mid, lo = split_bf16(jnp.concatenate([out[x][ri], out[x + 1][ri]], axis=1))
                 for p, part in enumerate((lo, hi, mid)):
-                    lhs[f, b, ri, OCT * x:OCT * x + HALF, LANES * p:LANES * p + LANES] = part
+                    lhs[:, ri, f, OCT * x:OCT * x + HALF, LANES * p:LANES * p + LANES] = part
 
     def field_x(f, src):
-        def body(b, carry):
-            to_x(f, b, lambda i: (merged[b, src * KEPT + i], merged[2 + b, src * KEPT + i]))
-            return carry
-        lax.fori_loop(0, 2, body, 0)
+        to_x(f, lambda i: (merged[RE, src * KEPT + i], merged[IM, src * KEPT + i]))
 
     def curl_x(f):
         c1, c2 = (f + 1) % 3, (f + 2) % 3
-
-        def body(b, carry):
-            ky, kz = (jnp.broadcast_to(wave[b, pl.ds(i, 1)], TILE) for i in PAIR)
-
-            def get(i):
-                ks = (UNIT * mode(SLOTS[i]), ky, kz)
-                m1, m2 = c1 * KEPT + i, c2 * KEPT + i
-                im = ks[c1] * merged[b, m2] - ks[c2] * merged[b, m1]
-                re = ks[c2] * merged[2 + b, m1] - ks[c1] * merged[2 + b, m2]
-                return re, im
-            to_x(3 + f, b, get)
-            return carry
-        lax.fori_loop(0, 2, body, 0)
+        ky, kz = wave[:, pl.ds(0, 1)], wave[:, pl.ds(1, 1)]
+
+        def get(i):
+            ks = (UNIT * mode(SLOTS[i]), ky, kz)
+            m1, m2 = c1 * KEPT + i, c2 * KEPT + i
+            im = ks[c1] * merged[RE, m2] - ks[c2] * merged[RE, m1]
+            re = ks[c2] * merged[IM, m1] - ks[c1] * merged[IM, m2]
+            return re, im
+        to_x(3 + f, get)
 
     def to_grid(f):
         sums = []
         for b in PAIR:
             parts = []
             for ri in PAIR:
-                low_hi, hi_mid = lhs[f, b, ri, :, 0:K], lhs[f, b, ri, :, LANES:LANES + K]
+                low_hi, hi_mid = lhs[b, ri, f, :, 0:K], lhs[b, ri, f, :, LANES:LANES + K]
                 acc = dot(low_hi, inv[b, ri, 0]) + dot(hi_mid, inv[b, ri, 1])
                 parts.append(acc + dot(hi_mid, inv[b, ri, 2]))
             sums.append((parts[0] + parts[1], parts[0] - parts[1]))
         for side in PAIR:
-            phys[f, 2 * side] = sums[0][side] + sums[1][side]
-            phys[f, 2 * side + 1] = sums[0][side] - sums[1][side]
+            phys[2 * side, f] = sums[0][side] + sums[1][side]
+            phys[2 * side + 1, f] = sums[0][side] - sums[1][side]
 
     def to_spec(c):
         for b in PAIR:
             for ri in PAIR:
-                hi, mid, lo = (prod[c, b, ri, p] for p in VEC)
+                hi, mid, lo = (prod[b, ri, p, c] for p in VEC)
                 both = dot(hi, fwd[b, ri, :, 0:K]) + dot(mid, fwd[b, ri, :, 0:K])
                 small = dot(lo, fwd[b, ri, :, 0:LANES]) + dot(hi, fwd[b, ri, :, K:])
-                spec[c, b, ri] = small + both[:, LANES:] + both[:, :LANES]
+                spec[b, ri, c] = small + both[:, LANES:] + both[:, :LANES]
 
     def product(c, point):
-        def body(i, carry):
-            rows = pl.ds(pl.multiple_of(i * HALF, HALF), HALF)
-            n = [point(q, rows) for q in FIELDS]
+        for at in range(0, K, FLOWS):
+            rows = slice(at, at + FLOWS)
+            n = [point(lambda f: phys[q, f, rows]) for q in FIELDS]
             for b in PAIR:
                 side = [n[0] - n[1], n[2] - n[3]] if b else [n[0] + n[1], n[2] + n[3]]
                 for ri in PAIR:
                     v = side[0] - side[1] if ri else side[0] + side[1]
                     for p, part in enumerate(split_bf16(v)):
-                        prod[c, b, ri, p, rows, :] = part
-            return carry
-        lax.fori_loop(0, HALF, body, 0, unroll=2)
+                        prod[b, ri, p, c, rows] = part
 
     def cross(c):
-        c1, c2 = (c + 1) % 3, (c + 2) % 3
-        product(c, lambda q, rows: phys[c1, q, rows, :] * phys[3 + c2, q, rows, :]
-                - phys[c2, q, rows, :] * phys[3 + c1, q, rows, :])
+        c1, c2 = lax.rem(c + 1, 3), lax.rem(c + 2, 3)
+        product(c, lambda at: at(c1) * at(3 + c2) - at(c2) * at(3 + c1))
 
     def flux(c):
-        product(c, lambda q, rows: phys[c, q, rows, :] * phys[6, q, rows, :])
+        product(c, lambda at: at(c) * at(6))
 
     def from_x(c):
-        def body(b, carry):
-            vals = [tuple(spec[c, b, ri, OCT * x:OCT * x + OCT, :] for ri in PAIR) for x in range(N)]
-            out = fft(vals, -1)
-            for i, j in enumerate(SLOTS):
-                for ri in PAIR:
-                    bins[c, 2 * ri + b, i] = out[j][ri]
-            return carry
-        lax.fori_loop(0, 2, body, 0)
-
-    def phase(b, re, im):
-        cos, sin = wave[b, pl.ds(2, 1)], wave[b, pl.ds(3, 1)]
+        vals = [tuple(spec[:, ri, c, OCT * x:OCT * x + OCT] for ri in PAIR) for x in range(N)]
+        out = fft(vals, -1)
+        for i, j in enumerate(SLOTS):
+            bins[c, RE, i], bins[c, IM, i] = out[j]
+
+    def phase(re, im):
+        cos, sin = wave[:, pl.ds(2, 1)], wave[:, pl.ds(3, 1)]
+        if re.ndim > 3:
+            cos, sin = cos[:, None], sin[:, None]
         return re * cos - im * sin, re * sin + im * cos
 
     def project():
-        def body(t, carry):
-            b, i = t // KEPT, t % KEPT
-            e = [home[pl.ds(t * 5 + k, 1)] for k in range(5)]
-            n = [[bins[c, 2 * ri + b, i] for c in VEC] for ri in PAIR]
-            one = [e[0] * n[ri][0] + e[1] * n[ri][1] for ri in PAIR]
-            two = [e[2] * n[ri][0] + e[3] * n[ri][1] + e[QUAD] * n[ri][2] for ri in PAIR]
+        for lo in range(0, KEPT, 7):
+            i = slice(lo, lo + 7)
+            e = [home[:, k, i] for k in range(5)]
+            n = [[bins[c, part, i] for c in VEC] for part in PARTS]
+            one = [e[0] * v[0] + e[1] * v[1] for v in n]
+            two = [e[2] * v[0] + e[3] * v[1] + e[QUAD] * v[2] for v in n]
             for which, v in enumerate((one, two)):
-                for ri, part in enumerate(phase(b, *v)):
-                    res[2 * ri + b, 2 * i + which] = part
-            return carry
-        lax.fori_loop(0, 2 * KEPT, body, 0, unroll=6)
+                for part, w in zip(PARTS, phase(*v)):
+                    res[part, which, i] = w
 
     def diverge():
-        def body(b, carry):
-            for i, j in enumerate(SLOTS):
-                ks = (UNIT * mode(j), wave[b, pl.ds(0, 1)], wave[b, pl.ds(1, 1)])
-                re, im = phase(b, *[sum(ks[c] * bins[c, 2 * ri + b, i] for c in VEC) for ri in PAIR])
-                res[b, 2 * KEPT + i] = im
-                res[2 + b, 2 * KEPT + i] = -re
-            for ri in PAIR:
-                res[2 * ri + b, 3 * KEPT] = jnp.zeros(TILE, F32)
-            return carry
-        lax.fori_loop(0, 2, body, 0)
+        for i, j in enumerate(SLOTS):
+            ks = (UNIT * mode(j), wave[:, pl.ds(0, 1)], wave[:, pl.ds(1, 1)])
+            re, im = phase(*[sum(ks[c] * bins[c, part, i] for c in VEC) for part in PARTS])
+            res[RE, 2, i] = im
+            res[IM, 2, i] = -re
+        res[:, 2, KEPT] = jnp.zeros((QUAD, *TILE), F32)
+
+    def result(n):
+        return res[:, n % 2, n // 2] if n < 2 * KEPT else res[:, 2, n - 2 * KEPT]
 
     def unmerge(lo, hi):
         p16 = lane % HALF
         zero = jnp.zeros(TILE, F32)
 
-        def body(rb, carry):
-            for t in range(lo, hi, 2):
-                ends = []
-                for h in PAIR:
-                    tiles = swap_blocks([res[rb, QUAD * (t + h) + s] for s in FIELDS], False)
-                    ret_d[0, t + h, rb], ret_d[1, t + h, rb] = tiles[:2]
-                    ret_d[2, t + h, rb] = jnp.where(low, tiles[2], zero)
-                    ret_d[3, t + h, rb] = jnp.where(low, roll(tiles[2], -2), zero)
-                    ends.append(tiles[3])
-                for o, (a, ok) in enumerate(((0, p16 < 12), (-QUAD, p16 >= OCT), (-20, (p16 < 12) & low), (-14, (p16 >= OCT) & low))):
-                    v = jnp.where(first_half, roll(ends[0], a) if a else ends[0], roll(ends[1], a + HALF))
-                    ret_s[o, t // 2, rb] = jnp.where(ok, v, zero)
-            return carry
-        lax.fori_loop(0, QUAD, body, 0)
+        for t in range(lo, hi, 2):
+            ends = []
+            for h in PAIR:
+                tiles = swap_blocks([result(QUAD * (t + h) + s) for s in FIELDS], False)
+                ret_d[0, t + h], ret_d[1, t + h] = tiles[:2]
+                ret_d[2, t + h] = jnp.where(low, tiles[2], zero)
+                ret_d[3, t + h] = jnp.where(low, roll(tiles[2], -2), zero)
+                ends.append(tiles[3])
+            for o, (a, ok) in enumerate(((0, p16 < 12), (-4, p16 >= 8), (-20, (p16 < 12) & low), (-14, (p16 >= 8) & low))):
+                v = jnp.where(first_half, roll(ends[0], a) if a else ends[0], roll(ends[1], a + HALF))
+                ret_s[o, t // 2] = jnp.where(ok, v, zero)
 
     def ret_part(kind, chunk):
         lo, hi = RET_CHUNKS[chunk], RET_CHUNKS[chunk + 1]
@@ -499,17 +483,20 @@
             curl_x(2)
             to_grid(1)
             to_grid(5)
-    curl_x(0)
-    curl_x(1)
-    for f in VEC:
-        to_grid(2 + f)
     tab[1].wait()
     tab[2].wait()
-    for c in VEC:
+    to_grid(2)
+    curl_x(0)
+    to_grid(3)
+    curl_x(1)
+    to_grid(QUAD)
+
+    @unrolled(3)
+    def _(c):
         cross(c)
-    for c in VEC:
         to_spec(c)
         from_x(c)
+
     project()
     for chunk in PAIR:
         unmerge(RET_CHUNKS[chunk], RET_CHUNKS[chunk + 1])
@@ -518,11 +505,13 @@
     merge(*bounds("D", 3))
     field_x(6, 3)
     to_grid(6)
-    for c in VEC:
+    def flux_part(c, carry):
         flux(c)
-    for c in VEC:
         to_spec(c)
         from_x(c)
+        return carry
+    lax.fori_loop(0, 3, flux_part, 0)
+
     diverge()
     unmerge(*RET_CHUNKS[2:])
     send_back(2)
@@ -665,9 +654,9 @@
             out_specs=hbm,
             scratch_shapes=[
                 pltpu.VMEM((2, QUAD * KEPT_ROWS + QUAD * FLOWS, FLOWS), F32), f32(OCT, D_OUT, QUAD), f32(QUAD, D_OUT, QUAD), f32(QUAD, S_OUT, QUAD),
-                f32(QUAD, QUAD * KEPT), pltpu.VMEM((7, 2, 2, K, 3 * LANES), BF16), pltpu.VMEM((7, QUAD, K, K), F32),
-                pltpu.VMEM((3, 2, 2, 3, K, K), BF16), pltpu.VMEM((3, 2, 2, K, LANES), F32), f32(3, QUAD, KEPT),
-                f32(QUAD, QUAD * D_RET), f32(QUAD, D_RET, QUAD), f32(QUAD, S_RET, QUAD),
+                f32(QUAD, QUAD * KEPT), pltpu.VMEM((2, 2, 7, K, 3 * LANES), BF16), pltpu.VMEM((QUAD, 7, K, K), F32),
+                pltpu.VMEM((2, 2, 3, 3, K, K), BF16), pltpu.VMEM((2, 2, 3, K, LANES), F32), f32(3, QUAD, KEPT),
+                f32(QUAD, 3, KEPT + 1), f32(QUAD, D_RET, QUAD), f32(QUAD, S_RET, QUAD),
                 pltpu.VMEM((2, 2, 3, K, K), BF16), *[pltpu.VMEM(a.shape, a.dtype) for a in consts[1:]],
                 dma((QUAD, 2, 2)), dma((9,)), dma((3,)), links, links, links, links,
             ],

time: 59.7 us -> 56.7 us (0.950)
  Pallas kernels: 58.6 us -> 55.6 us
    pallas_call x1, Pallas kernels: 53 us -> 50 us  [local_term(): pl.pallas_call(main_kernel, out_shape=jax.ShapeDtypeStruct((OCT, D_RET, Q...]
where the time goes in v4:
time: 56.7 us; the launch traced here: 56.4 us
  Pallas kernels  55.6 us (98%)
  between operations  0.8 us (1%)
    pallas_call x1, Pallas kernels, local_term(): pl.pallas_call(main_kernel, out_shape=jax.ShapeDtypeStruct((OCT, D_RET, Q...  50 us
    pallas_call x1, Pallas kernels, local_term(): pl.pallas_call(out_kernel, out_shape=[jax.ShapeDtypeStruct((c, ROWS, FLOW...  5.64 us

profile of v4, /device:TPU:1, one launch (start us, length us, event | category | flops | bytes accessed | tf_op | source)
XLA Modules:
  0.0 56.4 jit_solution(7860800355301522592)
XLA Ops:
  0.6 50.0 %flow_home.1.back_hbm = f32[8,16,4,8,128]{4,3,2,1,0:T(8,128)} custom-call(f32[3,2048,64]{2,1,0:T(8,128)} %bitcast.24, f32[3,2048,64]{2,1,0:T(8,128)} %bitcast.25, f32[1,2048,64]{2,1,0:T(8,128)} %bitcast.26, f32[1,2048,64]{2,1,0:T(8,128)} %bitcast.27, bf16[3,2,2,128,256]{4,3,2,1,0:T(8,128)(2,1)} %constant.10.clone.inv_hbm, ...), custom_call_target="tpu_custom_call" | custom-call | tf_op jit(solution)/shard_map/flow_home/pallas_call | solution.py:650
  50.6 5.6 %lay_out.1 = (f32[3,2048,64]{2,1,0:T(8,128)}, f32[3,2048,64]{2,1,0:T(8,128)}, f32[1,2048,64]{2,1,0:T(8,128)}, f32[1,2048,64]{2,1,0:T(8,128)}) custom-call(f32[8,16,4,8,128]{4,3,2,1,0:T(8,128)} %flow_home.1.back_hbm, f32[8,66,128]{2,1,0:T(8,128)} %constant.14.clone.tab_hbm), custom_call_target="tpu_custom_call" | custom-call | tf_op jit(solution)/shard_map/lay_out/pallas_call | solution.py:667

commit v5 on v4

v5 whole, which is shorter than its diff:
```python
import math

import jax
import jax.numpy as jnp
import numpy as np
from jax import lax
from jax.experimental import pallas as pl
from jax.experimental.pallas import tpu as pltpu
from jax.sharding import PartitionSpec as P

N = 32
LANES = 128
FLOWS = 64
ROWS = 2048
TILE = (8, LANES)
K = 256
TINY = 1e-9
MIB = 1 << 20
THREE, QUAD, SEVEN, OCT, HALF = 3, 4, 7, 8, 16
PARTS = RE, IM = slice(0, 2), slice(2, QUAD)
PAIR, VEC, FIELDS, PEERS = range(2), range(THREE), range(QUAD), range(1, OCT)
MESH = pl.DeviceIdType.MESH
F32 = jnp.float32
BF16 = jnp.bfloat16
UNIT = 2 * math.pi / N
SLOTS = list(range(11)) + list(range(22, N))
KEPT = len(SLOTS)
KEPT_ROWS = KEPT * FLOWS
LOW_ROWS = 11 * FLOWS
KINDS = {"D": (0, THREE), "A": (1,), "B": (2,)}
OUT = {"D": (N,) * 21, "A": (OCT, OCT, QUAD, OCT, QUAD, OCT, OCT, QUAD), "B": (OCT,) * 6}
RET = {"D": (N,) * HALF, "A": (OCT, OCT, QUAD, OCT, OCT, QUAD), "B": (OCT,) * QUAD}
OUT_EDGES = {"D": (0, 6, 11, HALF, 21), "A": (0, THREE, 5, 6, OCT), "B": (0, 2, THREE, QUAD, 6)}
RET_EDGES = {"D": (0, QUAD, 10, HALF), "A": (0, 1, THREE, 6), "B": (0, 1, 2, QUAD)}
SOURCES = [(kind, k * len(rows) + i, r, k) for kind, rows in KINDS.items() for k in PAIR for i, r in enumerate(rows)]


def units(kind, table, t):
    widths = table[kind]
    w = widths[t]
    per, nth = N // w, widths[:t].count(w)
    first = 48 if kind == "B" else HALF * (w == QUAD)
    out = []
    for s in FIELDS:
        for g in range(per):
            slot, start = QUAD * (per * nth + g) + s, first
            if slot >= QUAD * KEPT:
                slot, start = QUAD * (KEPT - 1) + s, first if kind == "B" else OCT * min(g - 5, 1)
            out.append((slot, N * s + w * g, w, start))
    return out


def place_of(kind, table, w, nth):
    return [t for t, v in enumerate(table[kind]) if v == w][nth]


def mode(j):
    return j if j < N // 2 else j - N


def kept(m):
    return THREE * abs(m) < N


def home_mode(lane, parity):
    block, p = divmod(lane, N)
    y, high, half = p // QUAD, p % QUAD // 2, p % QUAD
    if block < 2:
        row, col = THREE * block, 0
    elif block == 2:
        row, col, half = THREE * high, 1, p % 2
    elif p < 12:
        row, col = 1, 0
    elif p < 20:
        row, col, y = 2, 0, y + THREE
    else:
        row, col, half, y = 1 + high, 1, p % 2, y - 5 + 6 * high
    if y > SEVEN:
        return None
    ky, kz = mode(OCT * row + y), OCT * col + 2 * half + parity
    return (ky, kz) if kept(ky) and kept(kz) else None


def basis(kx, ky, kz):
    flat, full = math.hypot(kx, ky), math.hypot(kx, ky, kz)
    if full == 0:
        return np.zeros(THREE), np.zeros(THREE)
    if flat == 0:
        return np.array([1.0, 0, 0]), np.array([0, 1.0, 0])
    e1 = np.array([ky, -kx, 0]) / flat
    return e1, np.array([kx * kz, ky * kz, -flat * flat]) / (flat * full)


def split3(x):
    x = np.asarray(x, np.float32)
    hi = x.astype(BF16)
    rest = x - hi.astype(np.float32)
    mid = rest.astype(BF16)
    return hi, mid, (rest - mid.astype(np.float32)).astype(BF16)


def tables():
    scale = float(N) ** -1.5
    half = N // 2
    points = [(y, z) for z in range(1, OCT) for y in range(N)] + [(y, z) for z in (0, OCT) for y in range(half)]
    yy, zz = np.array(points).T
    inv = np.zeros((2, 2, LANES, K))
    wave = np.zeros((2, QUAD, LANES), np.float32)
    home = np.zeros((2, 5, KEPT, 1, LANES), np.float32)
    for parity in PAIR:
        for lane in range(LANES):
            got = home_mode(lane, parity)
            if got is None:
                continue
            ky, kz = got
            ang = UNIT * (ky * (yy + 0.5) + kz * zz)
            inv[parity, 0, lane] = scale * np.cos(ang)
            inv[parity, 1, lane] = -scale * np.sin(ang)
            wave[parity, :, lane] = ky * UNIT, kz * UNIT, math.cos(UNIT * ky / 2), math.sin(UNIT * ky / 2)
            for i, j in enumerate(SLOTS):
                e1, e2 = basis(mode(j), ky, kz)
                home[parity, :, i, 0, lane] = *e1[:2], *e2
    fwd = np.swapaxes(inv, 2, THREE)
    weight = np.full((2, 1, LANES, 1), 2.0)
    for lane in range(LANES):
        got = home_mode(lane, 0)
        if got is not None and got[1] == 0:
            weight[0, 0, lane] = 1.0
    inv3 = np.stack(split3(inv * weight))
    fwd3 = np.concatenate(split3(fwd), axis=THREE)
    return inv3, fwd3, wave, home


def source_tables():
    out = np.zeros((OCT, 2, HALF, THREE, LANES), np.float32)
    for kind, _, row, col in SOURCES:
        for t in range(len(RET[kind])):
            for n, lane, w, start in units(kind, RET, t):
                for o in range(w):
                    y, half = divmod(start // 2 + o, QUAD)
                    for parity in PAIR:
                        ky, kz = mode(OCT * row + y), OCT * col + 2 * half + parity
                        to = out[dev_of(row, col), parity, t, :, lane + o]
                        if n >= 2 * KEPT:
                            to[0] = 1
                        elif kept(ky) and kept(kz):
                            e1, e2 = basis(mode(SLOTS[n // 2]), ky, kz)
                            to[:] = (e2[1], e1[1], e2[2]) if n % 2 else (e1[0], e2[0], 0)
    return out.reshape(OCT, -1, LANES)


def cmul_const(a, c, s):
    re, im = a
    if abs(s) < TINY:
        return (re, im) if c > 0 else (-re, -im)
    if abs(c) < TINY:
        return (-im, re) if s > 0 else (im, -re)
    if abs(abs(c) - abs(s)) < TINY:
        p, q = (re - im) * abs(c), (re + im) * abs(c)
        if c > 0:
            return (p, q) if s > 0 else (q, -p)
        return (-q, p) if s > 0 else (-p, -q)
    return re * c - im * s, re * s + im * c


def fft(vals, sign):
    n = len(vals)
    if n == 1:
        return list(vals)
    even, odd = fft(vals[0::2], sign), fft(vals[1::2], sign)
    out = [None] * n
    for k in range(n // 2):
        a, b = even[k], odd[k]
        if b is not None:
            ang = sign * 2 * math.pi * k / n
            b = cmul_const(b, math.cos(ang), math.sin(ang))
        if a is None and b is None:
            continue
        if b is None:
            out[k], out[k + n // 2] = a, a
        elif a is None:
            out[k], out[k + n // 2] = b, (-b[0], -b[1])
        else:
            out[k] = (a[0] + b[0], a[1] + b[1])
            out[k + n // 2] = (a[0] - b[0], a[1] - b[1])
    return out


def dot(a, b):
    return jnp.dot(a, b, preferred_element_type=F32)


def split_bf16(x):
    hi = x.astype(BF16)
    rest = x - hi.astype(F32)
    mid = rest.astype(BF16)
    low = (rest - mid.astype(F32)).astype(BF16)
    return hi, mid, low


def dev_of(row, col):
    return col * QUAD + row


def kinds_here(row):
    tests = {"D": jnp.logical_or(row == 0, row == THREE), "A": row == 1, "B": row == 2}
    return list(tests.items())


def unrolled(n):
    def run(body):
        lax.fori_loop(0, n, lambda i, carry: (body(i), carry)[1], 0, unroll=True)
    return run


def roll(x, shift):
    shift %= LANES
    return pltpu.roll(x, shift, x.ndim - 1) if shift else x


def main_kernel(vre, vim, sre, sim, inv_hbm, fwd_hbm, wave_hbm, home_hbm, back,
                xin, send, recv_d, recv_a, recv_b, merged, lhs, phys, prod, spec, bins, res, ends, ret_d, ret_a, ret_b, stage,
                inv, fwd, wave, home, in_sem, tab_sem, own_sem, s1, r1, s2, r2):
    row, col, ens = lax.axis_index("row"), lax.axis_index("col"), lax.axis_index("ens")
    me = dev_of(row, col)
    recv = {"D": recv_d, "A": recv_a, "B": recv_b}
    ret = {"D": ret_d, "A": ret_a, "B": ret_b}
    mine = kinds_here(row)
    my_slot = {"D": col * 2 + jnp.where(row == THREE, 1, 0), "A": col, "B": col}

    loads = []
    for f in FIELDS:
        for ri in PAIR:
            src = (vre, vim)[ri].at[f] if f < THREE else (sre, sim)[ri].at[0]
            for half, (a, size, b) in enumerate(((0, LOW_ROWS, 0), (2 * LOW_ROWS, KEPT_ROWS - LOW_ROWS, LOW_ROWS))):
                cp = pltpu.make_async_copy(
                    src.at[pl.ds(a, size)], xin.at[ri, pl.ds(KEPT_ROWS * f + b, size)], in_sem.at[f, ri, half])
                cp.start()
                loads.append(cp)
    wanted = [(wave_hbm, wave), (fwd_hbm, fwd), (home_hbm, home)]
    wanted += [(inv_hbm.at[part], inv.at[:, :, pair, pl.ds(LANES * h, LANES)])
               for pair, parts in enumerate(((0, 2), (1, 1), (0, 0))) for h, part in enumerate(parts)]
    tab = [pltpu.make_async_copy(src, dst, tab_sem.at[i]) for i, (src, dst) in enumerate(wanted)]
    for cp in tab:
        cp.start()

    barrier = pltpu.get_barrier_semaphore()

    def peer(k):
        return row ^ (k % QUAD), col ^ (k // QUAD)

    for k in PEERS:
        pr, pc = peer(k)
        pl.semaphore_signal(barrier, inc=1, device_id=(ens, pc, pr), device_id_type=MESH)
    pl.semaphore_wait(barrier, SEVEN)

    def pack(kind, lo, hi):
        if kind == "D":
            def body(n, carry):
                t, rb = lax.div(n, QUAD), lax.rem(n, QUAD)
                blk = xin[lax.div(rb, 2), pl.ds(t * K + lax.rem(rb, 2), LANES, stride=2), :]
                send[:, t, rb] = blk.T.reshape(OCT, *TILE)
                return carry
            lax.fori_loop(QUAD * lo, QUAD * hi, body, 0, unroll=QUAD)
            return

        def few(rb, carry):
            ri, b = lax.div(rb, 2), lax.rem(rb, 2)
            for t in range(lo, hi):
                parts = [xin[ri, pl.ds(slot * FLOWS + start + b, w, stride=2), :] for slot, _, w, start in units(kind, OUT, t)]
                if OUT[kind][t] < OCT:
                    for (_, lane, w, _), part in zip(units(kind, OUT, t), parts):
                        stage[lane:lane + w, :] = part
                    blk = stage[...]
                else:
                    order = np.argsort([u[1] for u in units(kind, OUT, t)])
                    blk = jnp.concatenate([parts[i] for i in order], axis=0)
                send[:, t, rb] = blk.T.reshape(OCT, *TILE)
            return carry
        lax.fori_loop(0, QUAD, few, 0)

    def remote(src, dst, sems, i, j, chunk, r, c):
        return pltpu.make_async_remote_copy(
            src_ref=src, dst_ref=dst, send_sem=sems[0].at[i, chunk], recv_sem=sems[1].at[j, chunk],
            device_id=(ens, c, r), device_id_type=MESH)

    def out_copy(kind, chunk, slot, r, c, frm):
        lo, hi = OUT_EDGES[kind][chunk:chunk + 2]
        to = dev_of(r, c)
        part = pl.ds(lo, hi - lo)
        return remote(send.at[to, part], recv[kind].at[slot, part], (s1, r1), to, frm, chunk, r, c)

    for chunk in FIELDS:
        for cp in loads[OCT * chunk:OCT * chunk + OCT]:
            cp.wait()

        for kind, here in mine:
            @pl.when(here)
            def _():
                lo, hi = OUT_EDGES[kind][chunk:chunk + 2]
                pack(kind, lo, hi)
                for k in PEERS:
                    out_copy(kind, chunk, my_slot[kind], *peer(k), me).start()
                recv[kind][my_slot[kind], lo:hi] = send[me, lo:hi]

    lane = lax.broadcasted_iota(jnp.int32, TILE, 1)
    low = lane % QUAD < 2
    p32 = lane % N
    left, even = lane < FLOWS, lane % FLOWS < N

    def wait_chunk(chunk):
        for kind, slot, r, c in SOURCES:
            @pl.when(me != dev_of(r, c))
            def _():
                out_copy(kind, chunk, slot, r, c, dev_of(r, c)).wait_recv()

    def swap_blocks(tiles, forward):
        def outer(a, b, c, d):
            ca, db = roll(jnp.where(left, c, a), FLOWS), roll(jnp.where(left, d, b), FLOWS)
            return jnp.where(left, a, ca), jnp.where(left, b, db), jnp.where(left, ca, c), jnp.where(left, db, d)

        def inner(a, b, c, d):
            return (jnp.where(even, a, roll(b, N)), jnp.where(even, roll(a, -N), b),
                    jnp.where(even, c, roll(d, N)), jnp.where(even, roll(c, -N), d))
        return inner(*outer(*tiles)) if forward else outer(*inner(*tiles))

    def merge(lo, hi):
        cos, sin = wave[:, pl.ds(2, 1)], wave[:, pl.ds(THREE, 1)]
        for t in range(lo, hi):
            got = []
            for part in PARTS:
                d = [recv_d[o, t, part] for o in FIELDS]
                g, g4 = OCT * (t % QUAD), QUAD * (t % OCT)
                a4 = place_of("A", OUT, QUAD, t // OCT)
                a8, at = (a4, 20) if t == KEPT - 1 else (place_of("A", OUT, OCT, t // QUAD), g)
                c1 = jnp.where(low, d[2], roll(d[THREE], 2))
                v = [(roll(recv_a[c, a8, part], 20 * c - at), roll(recv_a[c, a4, part], 20 * c + OCT - g4),
                      roll(recv_b[c, t // QUAD, part], 10 * c + 12 - g)) for c in PAIR]
                rest = jnp.where(low, jnp.where(p32 < 28, v[1][0], v[1][1]), v[1][2])
                s1_ = jnp.where(p32 < OCT, v[0][0], jnp.where(p32 < 12, v[0][1], jnp.where(p32 < 20, v[0][2], rest)))
                got.append(swap_blocks((d[0], d[1], c1, s1_), True))
            for s, (re, im) in enumerate(zip(*got)):
                merged[RE, QUAD * t + s] = re * cos + im * sin
                merged[IM, QUAD * t + s] = im * cos - re * sin

    def to_x(f, get):
        vals = [None] * N
        for i, j in enumerate(SLOTS):
            vals[j] = get(i)
        out = fft(vals, 1)
        for x in range(0, N, 2):
            for ri in PAIR:
                hi, mid, lo = split_bf16(jnp.concatenate([out[x][ri], out[x + 1][ri]], axis=1))
                for p, part in enumerate((lo, hi, mid)):
                    lhs[:, ri, f, OCT * x:OCT * x + HALF, LANES * p:LANES * p + LANES] = part

    def field_x(f, src):
        to_x(f, lambda i: (merged[RE, src * KEPT + i], merged[IM, src * KEPT + i]))

    def curl_x(f):
        c1, c2 = (f + 1) % THREE, (f + 2) % THREE
        ky, kz = wave[:, pl.ds(0, 1)], wave[:, pl.ds(1, 1)]

        def get(i):
            ks = (UNIT * mode(SLOTS[i]), ky, kz)
            m1, m2 = c1 * KEPT + i, c2 * KEPT + i
            im = ks[c1] * merged[RE, m2] - ks[c2] * merged[RE, m1]
            re = ks[c2] * merged[IM, m1] - ks[c1] * merged[IM, m2]
            return re, im
        to_x(THREE + f, get)

    def to_grid(f):
        sums = []
        for b in PAIR:
            parts = []
            for ri in PAIR:
                low_hi, hi_mid = lhs[b, ri, f, :, 0:K], lhs[b, ri, f, :, LANES:LANES + K]
                acc = dot(low_hi, inv[b, ri, 0]) + dot(hi_mid, inv[b, ri, 1])
                parts.append(acc + dot(hi_mid, inv[b, ri, 2]))
            sums.append((parts[0] + parts[1], parts[0] - parts[1]))
        for side in PAIR:
            phys[2 * side, f] = sums[0][side] + sums[1][side]
            phys[2 * side + 1, f] = sums[0][side] - sums[1][side]

    def to_spec(c):
        for b in PAIR:
            for ri in PAIR:
                hi, mid, lo = (prod[b, ri, p, c] for p in VEC)
                both = dot(hi, fwd[b, ri, :, 0:K]) + dot(mid, fwd[b, ri, :, 0:K])
                small = dot(lo, fwd[b, ri, :, 0:LANES]) + dot(hi, fwd[b, ri, :, K:])
                spec[b, ri, c] = small + both[:, LANES:] + both[:, :LANES]

    def product(c, point):
        for at in range(0, K, FLOWS):
            rows = slice(at, at + FLOWS)
            n = [point(lambda f: phys[q, f, rows]) for q in FIELDS]
            for b in PAIR:
                side = [n[0] - n[1], n[2] - n[THREE]] if b else [n[0] + n[1], n[2] + n[THREE]]
                for ri in PAIR:
                    v = side[0] - side[1] if ri else side[0] + side[1]
                    for p, part in enumerate(split_bf16(v)):
                        prod[b, ri, p, c, rows] = part

    def cross(c):
        c1, c2 = lax.rem(c + 1, THREE), lax.rem(c + 2, THREE)
        product(c, lambda at: at(c1) * at(THREE + c2) - at(c2) * at(THREE + c1))

    def flux(c):
        product(c, lambda at: at(c) * at(6))

    def from_x(c):
        vals = [tuple(spec[:, ri, c, OCT * x:OCT * x + OCT] for ri in PAIR) for x in range(N)]
        out = fft(vals, -1)
        for i, j in enumerate(SLOTS):
            bins[c, RE, i], bins[c, IM, i] = out[j]

    def phase(re, im):
        cos, sin = wave[:, pl.ds(2, 1)], wave[:, pl.ds(THREE, 1)]
        if re.ndim > THREE:
            cos, sin = cos[:, None], sin[:, None]
        return re * cos - im * sin, re * sin + im * cos

    def project():
        for lo in range(0, KEPT, SEVEN):
            i = slice(lo, lo + SEVEN)
            e = [home[:, k, i] for k in range(5)]
            n = [[bins[c, part, i] for c in VEC] for part in PARTS]
            one = [e[0] * v[0] + e[1] * v[1] for v in n]
            two = [e[2] * v[0] + e[THREE] * v[1] + e[QUAD] * v[2] for v in n]
            for which, v in enumerate((one, two)):
                for part, w in zip(PARTS, phase(*v)):
                    res[part, which, i] = w

    def diverge():
        for i, j in enumerate(SLOTS):
            ks = (UNIT * mode(j), wave[:, pl.ds(0, 1)], wave[:, pl.ds(1, 1)])
            re, im = phase(*[sum(ks[c] * bins[c, part, i] for c in VEC) for part in PARTS])
            res[RE, 2, i] = im
            res[IM, 2, i] = -re
        res[:, 2, KEPT] = jnp.zeros((QUAD, *TILE), F32)

    def result(n):
        return res[:, n % 2, n // 2] if n < 2 * KEPT else res[:, 2, n - 2 * KEPT]

    def unmerge(chunk):
        zero = jnp.zeros(TILE, F32)
        for t in range(*RET_EDGES["D"][chunk:chunk + 2]):
            tiles = swap_blocks([result(QUAD * t + s) for s in FIELDS], False)
            ret_d[0, t], ret_d[1, t] = tiles[:2]
            ret_d[2, t] = jnp.where(low, tiles[2], zero)
            ret_d[THREE, t] = jnp.where(low, roll(tiles[2], -2), zero)
            ends[t] = tiles[THREE]
        for kind in "AB":
            for t in range(*RET_EDGES[kind][chunk:chunk + 2]):
                w = RET[kind][t]
                per, nth = N // w, RET[kind][:t].count(w)
                for c in PAIR:
                    first = 12 + 10 * c if kind == "B" else 20 * c + OCT * (w < OCT)
                    v = None
                    for g in range(per):
                        part = roll(ends[per * nth + g], w * g - first)
                        v = part if v is None else jnp.where(p32 >= w * g, part, v)
                    ret[kind][c, t] = jnp.where(low, v, zero) if c else v

    def ret_part(kind, chunk):
        lo, hi = RET_EDGES[kind][chunk:chunk + 2]
        return ret[kind], pl.ds(lo, hi - lo)

    def ret_copy(kind, chunk, slot, r, c, frm):
        src, part = ret_part(kind, chunk)
        return remote(src.at[slot, part], back.at[frm, part], (s2, r2), dev_of(r, c), frm, chunk, r, c)

    def own_copy(kind, chunk, slot, d):
        src, part = ret_part(kind, chunk)
        return pltpu.make_async_copy(src.at[slot, part], back.at[d, part], own_sem.at[chunk])

    def send_back(chunk):
        for kind, slot, r, c in SOURCES:
            d = dev_of(r, c)

            @pl.when(me != d)
            def _():
                ret_copy(kind, chunk, slot, r, c, me).start()

            @pl.when(me == d)
            def _():
                own_copy(kind, chunk, slot, d).start()

    tab[0].wait()
    for f in VEC:
        wait_chunk(f)
        merge(*OUT_EDGES["D"][f:f + 2])
        field_x(f, f)
        if f == 0:
            for cp in tab[THREE:]:
                cp.wait()
            to_grid(0)
        elif f == 1:
            curl_x(2)
            to_grid(1)
            to_grid(5)
    tab[1].wait()
    tab[2].wait()
    to_grid(2)
    curl_x(0)
    to_grid(THREE)
    curl_x(1)
    to_grid(QUAD)

    @unrolled(THREE)
    def _(c):
        cross(c)
        to_spec(c)
        from_x(c)

    project()
    for chunk in PAIR:
        unmerge(chunk)
        send_back(chunk)
    wait_chunk(THREE)
    merge(*OUT_EDGES["D"][THREE:])
    field_x(6, THREE)
    to_grid(6)
    def flux_part(c, carry):
        flux(c)
        to_spec(c)
        from_x(c)
        return carry
    lax.fori_loop(0, THREE, flux_part, 0)

    diverge()
    unmerge(2)
    send_back(2)

    for kind, here in mine:
        @pl.when(here)
        def _():
            for k in PEERS:
                pr, pc = peer(k)
                for chunk in FIELDS:
                    out_copy(kind, chunk, my_slot[kind], pr, pc, me).wait_send()
                for chunk in VEC:
                    ret_copy(kind, chunk, 0, pr, pc, dev_of(pr, pc)).wait_recv()

    for kind, slot, r, c in SOURCES:
        d = dev_of(r, c)

        @pl.when(me != d)
        def _():
            for chunk in VEC:
                ret_copy(kind, chunk, slot, r, c, me).wait_send()

        @pl.when(me == d)
        def _():
            for chunk in VEC:
                own_copy(kind, chunk, slot, d).wait()


def out_kernel(back_hbm, tab_hbm, ore, oim, tre, tim, buf, tab, back, blank, stage, sem, in_sem, tab_sem):
    row, col = lax.axis_index("row"), lax.axis_index("col")
    dense = kinds_here(row)[0][1]
    loads = [pltpu.make_async_copy(back_hbm.at[:, :, pl.ds(2 * ri, 2)], back.at[:, :, pl.ds(2 * ri, 2)], in_sem.at[ri])
             for ri in PAIR]
    load = pltpu.make_async_copy(tab_hbm.at[dev_of(row, col)], tab, tab_sem)
    for cp in (*loads, load):
        cp.start()
    odd = lax.broadcasted_iota(jnp.int32, (1, LANES), 1) % FLOWS >= N

    def store(f, ri, which):
        first = (0, LOW_ROWS, 2 * LOW_ROWS)[which]
        part = pl.ds(first, LOW_ROWS if which < 2 else ROWS - first)
        dst = (ore, oim)[ri].at[f] if f < THREE else (tre, tim)[ri].at[0]
        src = blank if which == 1 else buf.at[f, ri, part]
        return pltpu.make_async_copy(src, dst.at[part], sem.at[f, ri, which])

    blank[...] = jnp.zeros_like(blank)
    for f in FIELDS:
        for ri in PAIR:
            store(f, ri, 1).start()

    @pl.when(jnp.logical_not(dense))
    def _():
        for f in FIELDS:
            for ri in PAIR:
                for first, size in ((0, LOW_ROWS), (2 * LOW_ROWS, ROWS - 2 * LOW_ROWS)):
                    buf[f, ri, pl.ds(first, size), :] = jnp.zeros((size, FLOWS), F32)
    load.wait()

    def place(ri, b, kind, tile, t, shift, which):
        if RET[kind][t] < OCT:
            stage[...] = tile
        for n, lane, w, start in units(kind, RET, t):
            at = lane - N * shift
            if n < 2 * KEPT:
                if which and n % 2 == 0:
                    continue
                f, i = (2 if which else n % 2), n // 2
            elif which or n >= THREE * KEPT:
                continue
            else:
                f, i = THREE, n - 2 * KEPT
            part = stage[at:at + w, :] if w < OCT else tile[at:at + w]
            buf[f, ri, pl.ds(SLOTS[i] * FLOWS + b + start, w, stride=2), :] = part

    def rebuild(ri, kind):
        tiles = len(RET[kind])
        mixed = [t for t in range(tiles) if min(u[0] for u in units(kind, RET, t)) < 2 * KEPT]
        held = {}
        for t in range(tiles):
            for b in PAIR:
                v = back[:, t, 2 * ri + b].reshape(FLOWS, LANES)
                if t not in mixed:
                    place(ri, b, kind, v.T, t, 0, False)
                    continue
                k = [tab[pl.ds((b * HALF + t) * THREE + q, 1)] for q in VEC]
                other = jnp.where(odd, roll(v, N), roll(v, -N))
                place(ri, b, kind, (v * k[0] + other * k[1]).T, t, 0, False)
                z = v * k[2]
                if b in held:
                    old, zo = held.pop(b)
                    zt = jnp.where(odd, zo, roll(z, -N)).T
                    place(ri, b, kind, zt, old, 0, True)
                    place(ri, b, kind, zt, t, 1, True)
                elif t == mixed[-1]:
                    place(ri, b, kind, z.T, t, 0, True)
                else:
                    held[b] = t, z
            ends = (5, 10, 13, 15) if kind == "D" else ()
            if t in ends:
                e = ends.index(t)
                for f in VEC if e < 2 else (THREE,):
                    store(f, ri, 2 * (e % 2)).start()
        if kind != "D":
            for f in FIELDS:
                for which in (0, 2):
                    store(f, ri, which).start()

    for ri in PAIR:
        loads[ri].wait()

        for kind, here in kinds_here(row):
            @pl.when(here)
            def _():
                rebuild(ri, kind)
    for f in FIELDS:
        for ri in PAIR:
            for which in VEC:
                store(f, ri, which).wait()


def solution(mesh):
    spec_vec = P('ens', None, None, 'row', 'col')
    spec_scal = P('ens', None, 'row', 'col')
    consts = tables()
    src_np = source_tables()
    hbm = pl.BlockSpec(memory_space=pl.ANY)
    dma = pltpu.SemaphoreType.DMA
    links = dma((OCT, QUAD))

    def f32(*lead):
        return pltpu.VMEM((*lead, *TILE), F32)

    def local_term(vel_re, vel_im, scal_re, scal_im):
        vec = [jnp.transpose(a, (1, 2, THREE, QUAD, 0)).reshape(THREE, ROWS, FLOWS) for a in (vel_re, vel_im)]
        scal = [jnp.transpose(a, (1, 2, THREE, 0)).reshape(1, ROWS, FLOWS) for a in (scal_re, scal_im)]
        back = pl.pallas_call(
            main_kernel,
            out_shape=jax.ShapeDtypeStruct((OCT, HALF, QUAD, *TILE), F32),
            in_specs=[hbm] * OCT,
            out_specs=hbm,
            scratch_shapes=[
                pltpu.VMEM((2, QUAD * KEPT_ROWS, FLOWS), F32), f32(OCT, len(OUT["D"]), QUAD),
                *[f32(2 * len(rows), len(OUT[kind]), QUAD) for kind, rows in KINDS.items()],
                f32(QUAD, QUAD * KEPT), pltpu.VMEM((2, 2, SEVEN, K, THREE * LANES), BF16), pltpu.VMEM((QUAD, SEVEN, K, K), F32),
                pltpu.VMEM((2, 2, THREE, THREE, K, K), BF16), pltpu.VMEM((2, 2, THREE, K, LANES), F32), f32(THREE, QUAD, KEPT),
                f32(QUAD, THREE, KEPT + 1), f32(HALF, QUAD),
                *[f32(2 * len(rows), len(RET[kind]), QUAD) for kind, rows in KINDS.items()], pltpu.VMEM((LANES, FLOWS), F32),
                pltpu.VMEM((2, 2, THREE, K, K), BF16), *[pltpu.VMEM(a.shape, a.dtype) for a in consts[1:]],
                dma((QUAD, 2, 2)), dma((9,)), dma((THREE,)), links, links, links, links,
            ],
            compiler_params=pltpu.CompilerParams(
                collective_id=0, has_side_effects=True, vmem_limit_bytes=60 * MIB),
            name="flow_home",
        )(*vec, *scal, *[jnp.asarray(a) for a in consts])
        outs = pl.pallas_call(
            out_kernel,
            out_shape=[jax.ShapeDtypeStruct((c, ROWS, FLOWS), F32) for c in (THREE, THREE, 1, 1)],
            in_specs=[hbm, hbm],
            out_specs=[hbm] * QUAD,
            scratch_shapes=[pltpu.VMEM((QUAD, 2, ROWS, FLOWS), F32), pltpu.VMEM(src_np.shape[1:], F32),
                            f32(OCT, HALF, QUAD), pltpu.VMEM((LOW_ROWS, FLOWS), F32), pltpu.VMEM((LANES, FLOWS), F32), dma((QUAD, 2, THREE)), dma((2,)), dma],
            compiler_params=pltpu.CompilerParams(vmem_limit_bytes=60 * MIB),
            name="lay_out",
        )(back, jnp.asarray(src_np))
        out_v = [jnp.transpose(a.reshape(THREE, N, OCT, OCT, FLOWS), (QUAD, 0, 1, 2, THREE)) for a in outs[:2]]
        out_s = [jnp.transpose(a.reshape(N, OCT, OCT, FLOWS), (THREE, 0, 1, 2)) for a in outs[2:]]
        return (*out_v, *out_s)

    return jax.shard_map(local_term, mesh=mesh, in_specs=(spec_vec, spec_vec, spec_scal, spec_scal),
                         out_specs=(spec_vec, spec_vec, spec_scal, spec_scal), check_vma=False)
```

time: 56.7 us -> 53.3 us (0.940)
  Pallas kernels: 55.6 us -> 52.3 us
    pallas_call x1, Pallas kernels: 50 us -> 46.5 us  [local_term(): pl.pallas_call(main_kernel, out_shape=jax.ShapeDtypeStruct((OCT, HALF, QU...]
where the time goes in v5:
time: 53.3 us; the launch traced here: 53.1 us
  Pallas kernels  52.3 us (98%)
  between operations  0.8 us (2%)
    pallas_call x1, Pallas kernels, local_term(): pl.pallas_call(main_kernel, out_shape=jax.ShapeDtypeStruct((OCT, HALF, QU...  46.5 us
    pallas_call x1, Pallas kernels, local_term(): pl.pallas_call(out_kernel, out_shape=[jax.ShapeDtypeStruct((c, ROWS, FLOW...  5.8 us

profile of v5, /device:TPU:1, one launch (start us, length us, event | category | flops | bytes accessed | tf_op | source)
XLA Modules:
  0.0 53.1 jit_solution(11683453922305709440)
XLA Ops:
  0.6 46.5 %flow_home.1.back_hbm = f32[8,16,4,8,128]{4,3,2,1,0:T(8,128)} custom-call(f32[3,2048,64]{2,1,0:T(8,128)} %bitcast.24, f32[3,2048,64]{2,1,0:T(8,128)} %bitcast.25, f32[1,2048,64]{2,1,0:T(8,128)} %bitcast.26, f32[1,2048,64]{2,1,0:T(8,128)} %bitcast.27, bf16[3,2,2,128,256]{4,3,2,1,0:T(8,128)(2,1)} %constant.10.clone.inv_hbm, ...), custom_call_target="tpu_custom_call" | custom-call | tf_op jit(solution)/shard_map/flow_home/pallas_call | solution.py:666
  47.2 5.8 %lay_out.1 = (f32[3,2048,64]{2,1,0:T(8,128)}, f32[3,2048,64]{2,1,0:T(8,128)}, f32[1,2048,64]{2,1,0:T(8,128)}, f32[1,2048,64]{2,1,0:T(8,128)}) custom-call(f32[8,16,4,8,128]{4,3,2,1,0:T(8,128)} %flow_home.1.back_hbm, f32[8,96,128]{2,1,0:T(8,128)} %constant.14.clone.tab_hbm), custom_call_target="tpu_custom_call" | custom-call | tf_op jit(solution)/shard_map/lay_out/pallas_call | solution.py:685

commit v6 on v5

--- a/solution.py
+++ b/solution.py
@@ -235,15 +235,14 @@
             for half, (a, size, b) in enumerate(((0, LOW_ROWS, 0), (2 * LOW_ROWS, KEPT_ROWS - LOW_ROWS, LOW_ROWS))):
                 cp = pltpu.make_async_copy(
                     src.at[pl.ds(a, size)], xin.at[ri, pl.ds(KEPT_ROWS * f + b, size)], in_sem.at[f, ri, half])
-                cp.start()
                 loads.append(cp)
+    first, later = loads[:OCT], loads[OCT:]
+    for cp in first:
+        cp.start()
     wanted = [(wave_hbm, wave), (fwd_hbm, fwd), (home_hbm, home)]
     wanted += [(inv_hbm.at[part], inv.at[:, :, pair, pl.ds(LANES * h, LANES)])
                for pair, parts in enumerate(((0, 2), (1, 1), (0, 0))) for h, part in enumerate(parts)]
     tab = [pltpu.make_async_copy(src, dst, tab_sem.at[i]) for i, (src, dst) in enumerate(wanted)]
-    for cp in tab:
-        cp.start()
-
     barrier = pltpu.get_barrier_semaphore()
 
     def peer(k):
@@ -252,7 +251,6 @@
     for k in PEERS:
         pr, pc = peer(k)
         pl.semaphore_signal(barrier, inc=1, device_id=(ens, pc, pr), device_id_type=MESH)
-    pl.semaphore_wait(barrier, SEVEN)
 
     def pack(kind, lo, hi):
         if kind == "D":
@@ -277,7 +275,7 @@
                     blk = jnp.concatenate([parts[i] for i in order], axis=0)
                 send[:, t, rb] = blk.T.reshape(OCT, *TILE)
             return carry
-        lax.fori_loop(0, QUAD, few, 0)
+        lax.fori_loop(0, QUAD, few, 0, unroll=2)
 
     def remote(src, dst, sems, i, j, chunk, r, c):
         return pltpu.make_async_remote_copy(
@@ -291,14 +289,21 @@
         return remote(send.at[to, part], recv[kind].at[slot, part], (s1, r1), to, frm, chunk, r, c)
 
     for chunk in FIELDS:
-        for cp in loads[OCT * chunk:OCT * chunk + OCT]:
+        for cp in (first, later, (), ())[chunk]:
             cp.wait()
-
+        if chunk == 0:
+            for cp in (*later, *tab):
+                cp.start()
+        for kind, here in mine:
+            @pl.when(here)
+            def _():
+                pack(kind, *OUT_EDGES[kind][chunk:chunk + 2])
+        if chunk == 0:
+            pl.semaphore_wait(barrier, SEVEN)
         for kind, here in mine:
             @pl.when(here)
             def _():
                 lo, hi = OUT_EDGES[kind][chunk:chunk + 2]
-                pack(kind, lo, hi)
                 for k in PEERS:
                     out_copy(kind, chunk, my_slot[kind], *peer(k), me).start()
                 recv[kind][my_slot[kind], lo:hi] = send[me, lo:hi]

time: 53.3 us -> 52.8 us (level)
    pallas_call x1, Pallas kernels: 46.5 us -> 46 us  [local_term(): pl.pallas_call(main_kernel, out_shape=jax.ShapeDtypeStruct((OCT, HALF, QU...]
where the time goes in v6:
time: 52.8 us; the launch traced here: 52.6 us
  Pallas kernels  51.8 us (98%)
  between operations  0.8 us (2%)
    pallas_call x1, Pallas kernels, local_term(): pl.pallas_call(main_kernel, out_shape=jax.ShapeDtypeStruct((OCT, HALF, QU...  46 us
    pallas_call x1, Pallas kernels, local_term(): pl.pallas_call(out_kernel, out_shape=[jax.ShapeDtypeStruct((c, ROWS, FLOW...  5.8 us

profile of v6, /device:TPU:1, one launch (start us, length us, event | category | flops | bytes accessed | tf_op | source)
XLA Modules:
  0.0 52.6 jit_solution(4923179747968138995)
XLA Ops:
  0.6 46.0 %flow_home.1.back_hbm = f32[8,16,4,8,128]{4,3,2,1,0:T(8,128)} custom-call(f32[3,2048,64]{2,1,0:T(8,128)} %bitcast.24, f32[3,2048,64]{2,1,0:T(8,128)} %bitcast.25, f32[1,2048,64]{2,1,0:T(8,128)} %bitcast.26, f32[1,2048,64]{2,1,0:T(8,128)} %bitcast.27, bf16[3,2,2,128,256]{4,3,2,1,0:T(8,128)(2,1)} %constant.10.clone.inv_hbm, ...), custom_call_target="tpu_custom_call" | custom-call | tf_op jit(solution)/shard_map/flow_home/pallas_call | solution.py:671
  46.6 5.8 %lay_out.1 = (f32[3,2048,64]{2,1,0:T(8,128)}, f32[3,2048,64]{2,1,0:T(8,128)}, f32[1,2048,64]{2,1,0:T(8,128)}, f32[1,2048,64]{2,1,0:T(8,128)}) custom-call(f32[8,16,4,8,128]{4,3,2,1,0:T(8,128)} %flow_home.1.back_hbm, f32[8,96,128]{2,1,0:T(8,128)} %constant.14.clone.tab_hbm), custom_call_target="tpu_custom_call" | custom-call | tf_op jit(solution)/shard_map/lay_out/pallas_call | solution.py:690

commit v7 on v6

--- a/solution.py
+++ b/solution.py
@@ -32,6 +32,7 @@
 RET = {"D": (N,) * HALF, "A": (OCT, OCT, QUAD, OCT, OCT, QUAD), "B": (OCT,) * QUAD}
 OUT_EDGES = {"D": (0, 6, 11, HALF, 21), "A": (0, THREE, 5, 6, OCT), "B": (0, 2, THREE, QUAD, 6)}
 RET_EDGES = {"D": (0, QUAD, 10, HALF), "A": (0, 1, THREE, 6), "B": (0, 1, 2, QUAD)}
+BACK = [((0, 1), (0,)), ((1, 2), (0,)), ((0, 2), (1,)), ((2, THREE), (0, 1))]
 SOURCES = [(kind, k * len(rows) + i, r, k) for kind, rows in KINDS.items() for k in PAIR for i, r in enumerate(rows)]
 
 
@@ -275,7 +276,7 @@
                     blk = jnp.concatenate([parts[i] for i in order], axis=0)
                 send[:, t, rb] = blk.T.reshape(OCT, *TILE)
             return carry
-        lax.fori_loop(0, QUAD, few, 0, unroll=2)
+        lax.fori_loop(0, QUAD, few, 0)
 
     def remote(src, dst, sems, i, j, chunk, r, c):
         return pltpu.make_async_remote_copy(
@@ -387,8 +388,8 @@
             phys[2 * side, f] = sums[0][side] + sums[1][side]
             phys[2 * side + 1, f] = sums[0][side] - sums[1][side]
 
-    def to_spec(c):
-        for b in PAIR:
+    def to_spec(c, parities):
+        for b in parities:
             for ri in PAIR:
                 hi, mid, lo = (prod[b, ri, p, c] for p in VEC)
                 both = dot(hi, fwd[b, ri, :, 0:K]) + dot(mid, fwd[b, ri, :, 0:K])
@@ -413,48 +414,57 @@
     def flux(c):
         product(c, lambda at: at(c) * at(6))
 
-    def from_x(c):
-        vals = [tuple(spec[:, ri, c, OCT * x:OCT * x + OCT] for ri in PAIR) for x in range(N)]
+    def from_x(c, lo, hi):
+        vals = [tuple(spec[lo:hi, ri, c, OCT * x:OCT * x + OCT] for ri in PAIR) for x in range(N)]
         out = fft(vals, -1)
         for i, j in enumerate(SLOTS):
-            bins[c, RE, i], bins[c, IM, i] = out[j]
-
-    def phase(re, im):
-        cos, sin = wave[:, pl.ds(2, 1)], wave[:, pl.ds(THREE, 1)]
-        if re.ndim > THREE:
-            cos, sin = cos[:, None], sin[:, None]
+            bins[c, lo:hi, i], bins[c, lo + 2:hi + 2, i] = out[j]
+
+    def phase(re, im, b):
+        cos, sin = wave[b, pl.ds(2, 1)], wave[b, pl.ds(THREE, 1)]
         return re * cos - im * sin, re * sin + im * cos
 
-    def project():
+    def project(b):
         for lo in range(0, KEPT, SEVEN):
             i = slice(lo, lo + SEVEN)
-            e = [home[:, k, i] for k in range(5)]
-            n = [[bins[c, part, i] for c in VEC] for part in PARTS]
+            e = [home[b, k, i] for k in range(5)]
+            n = [[bins[c, 2 * ri + b, i] for c in VEC] for ri in PAIR]
             one = [e[0] * v[0] + e[1] * v[1] for v in n]
             two = [e[2] * v[0] + e[THREE] * v[1] + e[QUAD] * v[2] for v in n]
             for which, v in enumerate((one, two)):
-                for part, w in zip(PARTS, phase(*v)):
-                    res[part, which, i] = w
+                for ri, w in enumerate(phase(*v, b)):
+                    res[b, ri, which, i] = w
 
     def diverge():
         for i, j in enumerate(SLOTS):
             ks = (UNIT * mode(j), wave[:, pl.ds(0, 1)], wave[:, pl.ds(1, 1)])
-            re, im = phase(*[sum(ks[c] * bins[c, part, i] for c in VEC) for part in PARTS])
-            res[RE, 2, i] = im
-            res[IM, 2, i] = -re
-        res[:, 2, KEPT] = jnp.zeros((QUAD, *TILE), F32)
-
-    def result(n):
-        return res[:, n % 2, n // 2] if n < 2 * KEPT else res[:, 2, n - 2 * KEPT]
-
-    def unmerge(chunk):
+            re, im = phase(*[sum(ks[c] * bins[c, part, i] for c in VEC) for part in PARTS], slice(0, 2))
+            res[:, 0, 2, i] = im
+            res[:, 1, 2, i] = -re
+        res[:, :, 2, KEPT] = jnp.zeros((2, 2, *TILE), F32)
+
+    def result(n, b):
+        return res[b, :, n % 2, n // 2] if n < 2 * KEPT else res[b, :, 2, n - 2 * KEPT]
+
+    def unmerge(chunk, b):
         zero = jnp.zeros(TILE, F32)
-        for t in range(*RET_EDGES["D"][chunk:chunk + 2]):
-            tiles = swap_blocks([result(QUAD * t + s) for s in FIELDS], False)
-            ret_d[0, t], ret_d[1, t] = tiles[:2]
-            ret_d[2, t] = jnp.where(low, tiles[2], zero)
-            ret_d[THREE, t] = jnp.where(low, roll(tiles[2], -2), zero)
-            ends[t] = tiles[THREE]
+        def dense(t, four):
+            tiles = swap_blocks(four, False)
+            ret_d[0, t, b], ret_d[1, t, b] = tiles[:2]
+            ret_d[2, t, b] = jnp.where(low, tiles[2], zero)
+            ret_d[THREE, t, b] = jnp.where(low, roll(tiles[2], -2), zero)
+            ends[t, b] = tiles[THREE]
+
+        def two_components(t, carry):
+            dense(t, [res[b, :, s % 2, 2 * t + s // 2] for s in FIELDS])
+            return carry
+
+        lo, hi = RET_EDGES["D"][chunk:chunk + 2]
+        if chunk < 2:
+            lax.fori_loop(lo, hi, two_components, 0, unroll=2)
+        else:
+            for t in range(lo, hi):
+                dense(t, [result(QUAD * t + s, b) for s in FIELDS])
         for kind in "AB":
             for t in range(*RET_EDGES[kind][chunk:chunk + 2]):
                 w = RET[kind][t]
@@ -463,21 +473,22 @@
                     first = 12 + 10 * c if kind == "B" else 20 * c + OCT * (w < OCT)
                     v = None
                     for g in range(per):
-                        part = roll(ends[per * nth + g], w * g - first)
+                        part = roll(ends[per * nth + g, b], w * g - first)
                         v = part if v is None else jnp.where(p32 >= w * g, part, v)
-                    ret[kind][c, t] = jnp.where(low, v, zero) if c else v
+                    ret[kind][c, t, b] = jnp.where(low, v, zero) if c else v
 
     def ret_part(kind, chunk):
-        lo, hi = RET_EDGES[kind][chunk:chunk + 2]
-        return ret[kind], pl.ds(lo, hi - lo)
+        t, b = BACK[chunk]
+        lo, hi = (RET_EDGES[kind][i] for i in t)
+        return ret[kind], (pl.ds(lo, hi - lo), pl.ds(b[0], len(b)))
 
     def ret_copy(kind, chunk, slot, r, c, frm):
         src, part = ret_part(kind, chunk)
-        return remote(src.at[slot, part], back.at[frm, part], (s2, r2), dev_of(r, c), frm, chunk, r, c)
+        return remote(src.at[slot, *part], back.at[frm, *part], (s2, r2), dev_of(r, c), frm, chunk, r, c)
 
     def own_copy(kind, chunk, slot, d):
         src, part = ret_part(kind, chunk)
-        return pltpu.make_async_copy(src.at[slot, part], back.at[d, part], own_sem.at[chunk])
+        return pltpu.make_async_copy(src.at[slot, *part], back.at[d, *part], own_sem.at[chunk])
 
     def send_back(chunk):
         for kind, slot, r, c in SOURCES:
@@ -515,27 +526,38 @@
     @unrolled(THREE)
     def _(c):
         cross(c)
-        to_spec(c)
-        from_x(c)
-
-    project()
-    for chunk in PAIR:
-        unmerge(chunk)
-        send_back(chunk)
+        to_spec(c, (0,))
+        from_x(c, 0, 1)
+
+    def give(b):
+        project(b)
+        for chunk in PAIR:
+            unmerge(chunk, b)
+            if b + chunk != 1 or b == 0:
+                send_back(2 if b else chunk)
+
+    def second_parity(c, carry):
+        to_spec(c, (1,))
+        from_x(c, 1, 2)
+        return carry
+
+    give(0)
+    lax.fori_loop(0, THREE, second_parity, 0)
+    give(1)
     wait_chunk(THREE)
     merge(*OUT_EDGES["D"][THREE:])
     field_x(6, THREE)
     to_grid(6)
     def flux_part(c, carry):
         flux(c)
-        to_spec(c)
-        from_x(c)
+        to_spec(c, PAIR)
+        from_x(c, 0, 2)
         return carry
     lax.fori_loop(0, THREE, flux_part, 0)
 
     diverge()
-    unmerge(2)
-    send_back(2)
+    lax.fori_loop(0, 2, lambda b, carry: (unmerge(2, b), carry)[1], 0)
+    send_back(THREE)
 
     for kind, here in mine:
         @pl.when(here)
@@ -544,7 +566,7 @@
                 pr, pc = peer(k)
                 for chunk in FIELDS:
                     out_copy(kind, chunk, my_slot[kind], pr, pc, me).wait_send()
-                for chunk in VEC:
+                for chunk in range(len(BACK)):
                     ret_copy(kind, chunk, 0, pr, pc, dev_of(pr, pc)).wait_recv()
 
     for kind, slot, r, c in SOURCES:
@@ -552,19 +574,19 @@
 
         @pl.when(me != d)
         def _():
-            for chunk in VEC:
+            for chunk in range(len(BACK)):
                 ret_copy(kind, chunk, slot, r, c, me).wait_send()
 
         @pl.when(me == d)
         def _():
-            for chunk in VEC:
+            for chunk in range(len(BACK)):
                 own_copy(kind, chunk, slot, d).wait()
 
 
 def out_kernel(back_hbm, tab_hbm, ore, oim, tre, tim, buf, tab, back, blank, stage, sem, in_sem, tab_sem):
     row, col = lax.axis_index("row"), lax.axis_index("col")
     dense = kinds_here(row)[0][1]
-    loads = [pltpu.make_async_copy(back_hbm.at[:, :, pl.ds(2 * ri, 2)], back.at[:, :, pl.ds(2 * ri, 2)], in_sem.at[ri])
+    loads = [pltpu.make_async_copy(back_hbm.at[:, :, :, ri], back.at[:, :, :, ri], in_sem.at[ri])
              for ri in PAIR]
     load = pltpu.make_async_copy(tab_hbm.at[dev_of(row, col)], tab, tab_sem)
     for cp in (*loads, load):
@@ -613,7 +635,7 @@
         held = {}
         for t in range(tiles):
             for b in PAIR:
-                v = back[:, t, 2 * ri + b].reshape(FLOWS, LANES)
+                v = back[:, t, b, ri].reshape(FLOWS, LANES)
                 if t not in mixed:
                     place(ri, b, kind, v.T, t, 0, False)
                     continue
@@ -660,7 +682,7 @@
     src_np = source_tables()
     hbm = pl.BlockSpec(memory_space=pl.ANY)
     dma = pltpu.SemaphoreType.DMA
-    links = dma((OCT, QUAD))
+    links = dma((OCT, len(BACK)))
 
     def f32(*lead):
         return pltpu.VMEM((*lead, *TILE), F32)
@@ -670,7 +692,7 @@
         scal = [jnp.transpose(a, (1, 2, THREE, 0)).reshape(1, ROWS, FLOWS) for a in (scal_re, scal_im)]
         back = pl.pallas_call(
             main_kernel,
-            out_shape=jax.ShapeDtypeStruct((OCT, HALF, QUAD, *TILE), F32),
+            out_shape=jax.ShapeDtypeStruct((OCT, HALF, 2, 2, *TILE), F32),
             in_specs=[hbm] * OCT,
             out_specs=hbm,
             scratch_shapes=[
@@ -678,10 +700,10 @@
                 *[f32(2 * len(rows), len(OUT[kind]), QUAD) for kind, rows in KINDS.items()],
                 f32(QUAD, QUAD * KEPT), pltpu.VMEM((2, 2, SEVEN, K, THREE * LANES), BF16), pltpu.VMEM((QUAD, SEVEN, K, K), F32),
                 pltpu.VMEM((2, 2, THREE, THREE, K, K), BF16), pltpu.VMEM((2, 2, THREE, K, LANES), F32), f32(THREE, QUAD, KEPT),
-                f32(QUAD, THREE, KEPT + 1), f32(HALF, QUAD),
-                *[f32(2 * len(rows), len(RET[kind]), QUAD) for kind, rows in KINDS.items()], pltpu.VMEM((LANES, FLOWS), F32),
+                f32(2, 2, THREE, KEPT + 1), f32(HALF, 2, 2),
+                *[f32(2 * len(rows), len(RET[kind]), 2, 2) for kind, rows in KINDS.items()], pltpu.VMEM((LANES, FLOWS), F32),
                 pltpu.VMEM((2, 2, THREE, K, K), BF16), *[pltpu.VMEM(a.shape, a.dtype) for a in consts[1:]],
-                dma((QUAD, 2, 2)), dma((9,)), dma((THREE,)), links, links, links, links,
+                dma((QUAD, 2, 2)), dma((9,)), dma((len(BACK),)), links, links, links, links,
             ],
             compiler_params=pltpu.CompilerParams(
                 collective_id=0, has_side_effects=True, vmem_limit_bytes=60 * MIB),
@@ -693,7 +715,7 @@
             in_specs=[hbm, hbm],
             out_specs=[hbm] * QUAD,
             scratch_shapes=[pltpu.VMEM((QUAD, 2, ROWS, FLOWS), F32), pltpu.VMEM(src_np.shape[1:], F32),
-                            f32(OCT, HALF, QUAD), pltpu.VMEM((LOW_ROWS, FLOWS), F32), pltpu.VMEM((LANES, FLOWS), F32), dma((QUAD, 2, THREE)), dma((2,)), dma],
+                            f32(OCT, HALF, 2, 2), pltpu.VMEM((LOW_ROWS, FLOWS), F32), pltpu.VMEM((LANES, FLOWS), F32), dma((QUAD, 2, THREE)), dma((2,)), dma],
             compiler_params=pltpu.CompilerParams(vmem_limit_bytes=60 * MIB),
             name="lay_out",
         )(back, jnp.asarray(src_np))

time: 52.8 us -> 52.5 us (level)
  no operation moved by 1% of the time
where the time goes in v7:
time: 52.5 us; the launch traced here: 52.3 us
  Pallas kernels  51.5 us (98%)
  between operations  0.8 us (2%)
    pallas_call x1, Pallas kernels, local_term(): pl.pallas_call(main_kernel, out_shape=jax.ShapeDtypeStruct((OCT, HALF, 2,...  45.7 us
    pallas_call x1, Pallas kernels, local_term(): pl.pallas_call(out_kernel, out_shape=[jax.ShapeDtypeStruct((c, ROWS, FLOW...  5.8 us

profile of v7, /device:TPU:1, one launch (start us, length us, event | category | flops | bytes accessed | tf_op | source)
XLA Modules:
  0.0 52.3 jit_solution(14092916050666929701)
XLA Ops:
  0.6 45.7 %flow_home.1.back_hbm = f32[8,16,2,2,8,128]{5,4,3,2,1,0:T(8,128)} custom-call(f32[3,2048,64]{2,1,0:T(8,128)} %bitcast.24, f32[3,2048,64]{2,1,0:T(8,128)} %bitcast.25, f32[1,2048,64]{2,1,0:T(8,128)} %bitcast.26, f32[1,2048,64]{2,1,0:T(8,128)} %bitcast.27, bf16[3,2,2,128,256]{4,3,2,1,0:T(8,128)(2,1)} %constant.10.clone.inv_hbm, ...), custom_call_target="tpu_custom_call" | custom-call | tf_op jit(solution)/shard_map/flow_home/pallas_call | solution.py:693
  46.3 5.8 %lay_out.1 = (f32[3,2048,64]{2,1,0:T(8,128)}, f32[3,2048,64]{2,1,0:T(8,128)}, f32[1,2048,64]{2,1,0:T(8,128)}, f32[1,2048,64]{2,1,0:T(8,128)}) custom-call(f32[8,16,2,2,8,128]{5,4,3,2,1,0:T(8,128)} %flow_home.1.back_hbm, f32[8,96,128]{2,1,0:T(8,128)} %constant.14.clone.tab_hbm), custom_call_target="tpu_custom_call" | custom-call | tf_op jit(solution)/shard_map/lay_out/pallas_call | solution.py:712

commit v8 on v7

--- a/solution.py
+++ b/solution.py
@@ -260,7 +260,7 @@
                 blk = xin[lax.div(rb, 2), pl.ds(t * K + lax.rem(rb, 2), LANES, stride=2), :]
                 send[:, t, rb] = blk.T.reshape(OCT, *TILE)
                 return carry
-            lax.fori_loop(QUAD * lo, QUAD * hi, body, 0, unroll=QUAD)
+            lax.fori_loop(QUAD * lo, QUAD * hi, body, 0, unroll=2)
             return
 
         def few(rb, carry):
@@ -461,7 +461,7 @@
 
         lo, hi = RET_EDGES["D"][chunk:chunk + 2]
         if chunk < 2:
-            lax.fori_loop(lo, hi, two_components, 0, unroll=2)
+            lax.fori_loop(lo, hi, two_components, 0, unroll=2 if chunk else QUAD)
         else:
             for t in range(lo, hi):
                 dense(t, [result(QUAD * t + s, b) for s in FIELDS])

time: 52.5 us -> 52.2 us (level)
  no operation moved by 1% of the time
where the time goes in v8:
time: 52.2 us; the launch traced here: 52 us
  Pallas kernels  51.2 us (98%)
  between operations  0.8 us (2%)
    pallas_call x1, Pallas kernels, local_term(): pl.pallas_call(main_kernel, out_shape=jax.ShapeDtypeStruct((OCT, HALF, 2,...  45.4 us
    pallas_call x1, Pallas kernels, local_term(): pl.pallas_call(out_kernel, out_shape=[jax.ShapeDtypeStruct((c, ROWS, FLOW...  5.8 us

profile of v8, /device:TPU:1, one launch (start us, length us, event | category | flops | bytes accessed | tf_op | source)
XLA Modules:
  0.0 52.0 jit_solution(1191605332409234898)
XLA Ops:
  0.6 45.4 %flow_home.1.back_hbm = f32[8,16,2,2,8,128]{5,4,3,2,1,0:T(8,128)} custom-call(f32[3,2048,64]{2,1,0:T(8,128)} %bitcast.24, f32[3,2048,64]{2,1,0:T(8,128)} %bitcast.25, f32[1,2048,64]{2,1,0:T(8,128)} %bitcast.26, f32[1,2048,64]{2,1,0:T(8,128)} %bitcast.27, bf16[3,2,2,128,256]{4,3,2,1,0:T(8,128)(2,1)} %constant.10.clone.inv_hbm, ...), custom_call_target="tpu_custom_call" | custom-call | tf_op jit(solution)/shard_map/flow_home/pallas_call | solution.py:693
  46.0 5.8 %lay_out.1 = (f32[3,2048,64]{2,1,0:T(8,128)}, f32[3,2048,64]{2,1,0:T(8,128)}, f32[1,2048,64]{2,1,0:T(8,128)}, f32[1,2048,64]{2,1,0:T(8,128)}) custom-call(f32[8,16,2,2,8,128]{5,4,3,2,1,0:T(8,128)} %flow_home.1.back_hbm, f32[8,96,128]{2,1,0:T(8,128)} %constant.14.clone.tab_hbm), custom_call_target="tpu_custom_call" | custom-call | tf_op jit(solution)/shard_map/lay_out/pallas_call | solution.py:712
